TPU v7x, 32 devices: a whole 2x2x4 slice. The times are simulated.
32 devices in a mesh: dp: 4 (over x, core), tm: 2 (over y), height: 4 (over z).
Axes of the slice: x: 2, y: 2, z: 4, core: 2. Of those that a mesh axis runs over, the one named last changes fastest.
Arguments:
- latent: bfloat16 [16, 8, 16, 512], P(('dp', 'tm'), None, None, 'height'), parts along dimension 0, may hold values from -6 to 6
- gain_latent: float32 [512], P('height'), may hold values from 0.25 to 1.75
- shift_latent: float32 [512], P('height'), may hold values from -3 to 3
- conv_latent: bfloat16 [13824, 512], P('tm', 'height'), may hold values from -0.0546875 to 0.0546875
- up_weight: bfloat16 [512, 2048], P('height'), may hold values from -0.25 to 0.25
- gain_block: float32 [256], replicated, may hold values from 0.25 to 1.75
- shift_block: float32 [256], replicated, may hold values from -3 to 3
- conv_block: bfloat16 [6912, 256], P(('tm', 'height')), may hold values from -0.078125 to 0.078125
- cotangent: bfloat16 [32, 16, 32, 256], P(('dp', 'tm'), 'height'), parts along dimension 0, may hold values from -6 to 6
Outputs:
- decoded: bfloat16 [32, 16, 32, 256], P(('dp', 'tm'), 'height'), parts along dimension 0
- grad_upsampled: bfloat16 [32, 16, 32, 256], P(('dp', 'tm'), 'height'), parts along dimension 0
- grad_weight: float32 [9216, 256], P(('dp', 'tm', 'height')), parts along dimension 0
- grad_gain: float32 [1024], P('dp'), parts along dimension 0
- grad_shift: float32 [1024], P('dp'), parts along dimension 0
There are 4 independent parts, one for each index of `dp`. A program takes and returns all parts, laid end to end along the dimension named above; an argument that names none is the same for every part. Nothing has to cross between parts.
All inputs are finite; a program needn't handle non-finite values.
Results may differ from a plain program's by a relative error of at most 0.009.
Values may be sent and summed in bfloat16 or wider, within the bound.
A program may use at most 128 MiB of HBM per device.

v0:
```python
import functools

import jax
import jax.numpy as jnp
from jax import lax
from jax.experimental import pallas as pl
from jax.experimental.pallas import tpu as pltpu
from jax.sharding import PartitionSpec as P

C1 = 512
GROUPS = 32


epsilon = 1e-06


def shifted(block, axis, distance):
    devices = range(lax.axis_size(axis))
    route = [(i - distance, i) for i in devices if i - distance in devices]
    return lax.ppermute(block, axis, route)


def extended_2(cells, sides, width):
    for axis, dim in sides:
        count = lax.axis_size(axis)
        ends = count - 1
        head = lax.slice_in_dim(cells, 0, width, axis=dim)
        tail = lax.slice_in_dim(cells, cells.shape[dim] - width, cells.shape[dim], axis=dim)
        cells = jnp.concatenate(
            [
                lax.ppermute(tail, axis, [(i, (i + 1) % count) for i in range(ends)]),
                cells,
                lax.ppermute(head, axis, [((i + 1) % count, i) for i in range(ends)]),
            ],
            axis=dim,
        )
    return cells


def standardize(values, mean_value, inverse, groups):
    shape_full = values.shape
    grouped = values.reshape(shape_full[:-1] + (groups, shape_full[-1] // groups))
    return ((grouped - mean_value[:, None]) * inverse[:, None]).reshape(shape_full)


def causal_taps(padded, weight, frames, rows, cols):
    channels_in = padded.shape[-1]
    summed = jnp.zeros((frames * rows * cols, weight.shape[1]), jnp.float32)
    for lag_step in range(3):
        for row_step in range(3):
            for col_step in range(3):
                tap_index = (lag_step * 3 + row_step) * 3 + col_step
                window = padded[
                    lag_step : lag_step + frames,
                    row_step : row_step + rows,
                    col_step : col_step + cols,
                ]
                kernel = weight[tap_index * channels_in : (tap_index + 1) * channels_in]
                summed = summed + jnp.dot(
                    window.reshape(-1, channels_in), kernel, preferred_element_type=jnp.float32
                )
    return summed.reshape(frames, rows, cols, weight.shape[1])


def transposed_taps(padded, weight, frames, rows, cols):
    channels_out = padded.shape[-1]
    channels_in = weight.shape[0] // 27
    summed = jnp.zeros((frames * rows * cols, channels_in), jnp.float32)
    for lag_step in range(3):
        for row_step in range(3):
            for col_step in range(3):
                tap_index = (lag_step * 3 + row_step) * 3 + col_step
                window = padded[
                    2 - lag_step : 2 - lag_step + frames,
                    2 - row_step : 2 - row_step + rows,
                    2 - col_step : 2 - col_step + cols,
                ]
                kernel = weight[tap_index * channels_in : (tap_index + 1) * channels_in]
                summed = summed + lax.dot_general(
                    window.reshape(-1, channels_out),
                    kernel,
                    (((1,), (1,)), ((), ())),
                    preferred_element_type=jnp.float32,
                )
    return summed.reshape(frames, rows, cols, channels_in)


def weight_terms(padded, grads, frames, rows, cols):
    channels_in = padded.shape[-1]
    flat_grads = grads.reshape(-1, grads.shape[-1])
    blocks = []
    for row_step in range(3):
        for col_step in range(3):
            window = padded[2 : 2 + frames, row_step : row_step + rows, col_step : col_step + cols]
            blocks.append(
                lax.dot_general(
                    window.reshape(-1, channels_in),
                    flat_grads,
                    (((0,), (0,)), ((), ())),
                    preferred_element_type=jnp.float32,
                )
            )
    return jnp.concatenate(blocks, 0)


def local(
    latent,
    gain_latent,
    shift_latent,
    conv_latent,
    up_weight,
    gain_block,
    shift_block,
    conv_block,
    cotangent,
):
    per_group = C1 // GROUPS
    groups_here = latent.shape[-1] // per_group
    latent_f32 = latent.astype(jnp.float32)
    grouped = latent_f32.reshape(-1, groups_here, per_group)
    first_sums = jnp.sum(grouped, axis=(0, 2))
    second_sums = jnp.sum(grouped * grouped, axis=(0, 2))
    first_totals, second_totals = lax.psum((first_sums, second_sums), "tm")
    count_latent = grouped.shape[0] * per_group * lax.axis_size("tm")
    mean_latent = first_totals / count_latent
    inverse_latent = lax.rsqrt(second_totals / count_latent - mean_latent * mean_latent + epsilon)
    normed = (
        standardize(latent_f32, mean_latent, inverse_latent, groups_here) * gain_latent
        + shift_latent
    )
    active = jax.nn.silu(normed).astype(jnp.bfloat16)
    earlier = shifted(active, "tm", 1)
    extended = jnp.concatenate([earlier, active], 0)
    all_channels = lax.all_gather(extended, "height", axis=3, tiled=True)
    padded = jnp.pad(all_channels, ((0, 0), (1, 1), (1, 1), (0, 0)))
    latent_weight = lax.all_gather(conv_latent, "tm", axis=0, tiled=True)
    frames_latent, rows_latent, cols_latent = (latent.shape[0], latent.shape[1], latent.shape[2])
    mixed = causal_taps(padded, latent_weight, frames_latent, rows_latent, cols_latent)
    refined = (latent_f32 + mixed).astype(jnp.bfloat16)
    band_rows = rows_latent // lax.axis_size("height")
    own_band = lax.all_to_all(refined, "height", split_axis=1, concat_axis=3, tiled=True)
    flat_band = own_band.reshape(-1, own_band.shape[-1])
    expanded = jnp.dot(
        flat_band,
        lax.all_gather(up_weight, "height", axis=0, tiled=True),
        preferred_element_type=jnp.float32,
    )
    channels_block = up_weight.shape[1] // 8
    spread = expanded.reshape(frames_latent, band_rows, cols_latent, 2, 2, 2, channels_block)
    spread = spread.transpose(0, 3, 1, 4, 2, 5, 6)
    upsampled = spread.reshape(
        2 * frames_latent, 2 * band_rows, 2 * cols_latent, channels_block
    ).astype(jnp.bfloat16)
    frames_block, rows_block, cols_block = (
        upsampled.shape[0],
        upsampled.shape[1],
        upsampled.shape[2],
    )
    up_f32 = upsampled.astype(jnp.float32)
    per_block = channels_block // GROUPS
    grouped_block = up_f32.reshape(-1, GROUPS, per_block)
    block_first = jnp.sum(grouped_block, axis=(0, 2))
    block_second = jnp.sum(grouped_block * grouped_block, axis=(0, 2))
    block_first, block_second = lax.psum((block_first, block_second), ("tm", "height"))
    count_block = grouped_block.shape[0] * per_block * lax.axis_size("tm") * lax.axis_size("height")
    mean_block = block_first / count_block
    inverse_block = lax.rsqrt(block_second / count_block - mean_block * mean_block + epsilon)
    standard = standardize(up_f32, mean_block, inverse_block, GROUPS)
    normed_block = standard * gain_block + shift_block
    active_block = jax.nn.silu(normed_block).astype(jnp.bfloat16)
    before = shifted(active_block[-2:], "tm", 1)
    ext_block = jnp.concatenate([before, active_block], 0)
    beside_all = extended_2(ext_block, (("height", 1),), 1)
    padded_block = jnp.pad(beside_all, ((0, 0), (0, 0), (1, 1), (0, 0)))
    block_weight = lax.all_gather(conv_block, ("tm", "height"), axis=0, tiled=True)
    mixed_block = causal_taps(padded_block, block_weight, frames_block, rows_block, cols_block)
    decoded = (up_f32 + mixed_block).astype(jnp.bfloat16)
    after = shifted(cotangent[:2], "tm", -1)
    grad_ext = jnp.concatenate([cotangent, after], 0)
    grad_around = extended_2(grad_ext, (("height", 1),), 1)
    grad_padded = jnp.pad(grad_around, ((0, 0), (0, 0), (1, 1), (0, 0)))
    grad_active = transposed_taps(grad_padded, block_weight, frames_block, rows_block, cols_block)
    local_terms = weight_terms(padded_block, cotangent, frames_block, rows_block, cols_block)
    grad_weight = lax.psum_scatter(local_terms, ("tm", "height"), scatter_dimension=0, tiled=True)
    sigmoid = jax.nn.sigmoid(normed_block)
    grad_normed = grad_active * sigmoid * (1.0 + normed_block * (1.0 - sigmoid))
    flat_grad = grad_normed.reshape(-1, channels_block)
    flat_standard = standard.reshape(-1, channels_block)
    grad_shift, grad_gain = lax.psum(
        (jnp.sum(flat_grad, axis=0), jnp.sum(flat_grad * flat_standard, axis=0)), ("tm", "height")
    )
    first_mean = jnp.sum((gain_block * grad_shift).reshape(GROUPS, per_block), axis=1) / count_block
    second_mean = jnp.sum((gain_block * grad_gain).reshape(GROUPS, per_block), axis=1) / count_block
    grouped_grad = (grad_normed * gain_block).reshape(-1, GROUPS, per_block)
    grouped_standard = standard.reshape(-1, GROUPS, per_block)
    corrected = (
        grouped_grad - first_mean[:, None] - grouped_standard * second_mean[:, None]
    ) * inverse_block[:, None]
    grad_upsampled = (cotangent.astype(jnp.float32) + corrected.reshape(cotangent.shape)).astype(
        jnp.bfloat16
    )
    return (decoded, grad_upsampled, grad_weight, grad_gain, grad_shift)


MESH = pl.DeviceIdType.MESH
F32 = jnp.float32
BF16 = jnp.bfloat16


def group_matrix(channels, per):
    row = lax.broadcasted_iota(jnp.int32, (channels, channels), 0) // per
    col = lax.broadcasted_iota(jnp.int32, (channels, channels), 1) // per
    return (row == col).astype(F32)


def over_groups(rows, per):
    return jnp.dot(
        rows,
        group_matrix(rows.shape[-1], per),
        precision=lax.Precision.HIGHEST,
        preferred_element_type=F32,
    )


def column_shift(cells, cols, step):
    count = cells.shape[0]
    column = lax.broadcasted_iota(jnp.int32, cells.shape, 0) % cols
    edge = 0 if step == 1 else cols - 1
    return jnp.where(column == edge, 0.0, pltpu.roll(cells, step % count, 0))


def two_rows(first, second):
    width = first.shape[-1]
    row = lax.broadcasted_iota(jnp.int32, (8, width), 0)
    return jnp.where(row == 0, first, jnp.where(row == 1, second, 0.0))


def block_kernel(sizes, n_send, *refs):
    (T, H, Fl, Rl, Cl, CH, C2, F, R, C) = sizes
    (
        latent, gain_l, shift_l, w_l, up_w, gain_b, shift_b, w_b, cot,
        decoded, grad_up, grad_w, grad_gs,
        act, abuf, acc_l, part, parts_in, stat1, stat2, stat3, upw, wb,
        upf, std, ab, cb, cot3, gw, gy, gs, gz, acc, lace, send_sem, recv_sem, local_sem,
    ) = refs
    d, t, h = lax.axis_index("dp"), lax.axis_index("tm"), lax.axis_index("height")
    N = T * H
    FL = T * Fl
    U = H * CH // T
    band = Rl // H
    pair = d + 1 - 2 * (d % 2)
    half = d % 2
    used = [0]
    sent = []

    def at(kt, kh):
        return (d, lax.rem(t + kt, T), lax.rem(h + kh, H))

    def copy(src, dst, device):
        k = used[0]
        used[0] += 1
        return pltpu.make_async_remote_copy(
            src_ref=src, dst_ref=dst, send_sem=send_sem.at[k], recv_sem=recv_sem.at[k],
            device_id=device, device_id_type=MESH,
        )

    def go(src, dst, device):
        made = copy(src, dst, device)
        made.start()
        sent.append(made)
        return made

    peers = [(kt, kh) for kt in range(T) for kh in range(H) if kt or kh]

    abuf[...] = jnp.zeros(abuf.shape, BF16)
    ab[...] = jnp.zeros(ab.shape, BF16)
    cb[...] = jnp.zeros(cb.shape, BF16)

    barrier = pltpu.get_barrier_semaphore()
    for kt, kh in peers:
        pl.semaphore_signal(barrier, inc=1, device_id=at(kt, kh), device_id_type=MESH)
    pl.semaphore_signal(barrier, inc=1, device_id=(pair, t, h), device_id_type=MESH)
    pl.semaphore_wait(barrier, N)

    x = latent[...].astype(F32).reshape(Fl * Rl * Cl, CH)
    stat1[t] = two_rows(jnp.sum(x, 0, keepdims=True), jnp.sum(x * x, 0, keepdims=True))
    s1 = [go(stat1.at[t], stat1.at[t], at(kt, 0)) for kt in range(1, T)]
    cb[0:F, 1 : 1 + R] = cot[...]
    wide = cot[...].astype(F32).reshape(F * R * C, C2)
    cot3[:, 0:C2] = column_shift(wide, C, -1).astype(BF16)
    cot3[:, C2 : 2 * C2] = cot[...].reshape(F * R * C, C2)
    cot3[:, 2 * C2 :] = column_shift(wide, C, 1).astype(BF16)
    for made in s1:
        made.wait_recv()
    per_l = H * CH // GROUPS
    count_l = FL * Rl * Cl * per_l
    total = stat1[0]
    for k in range(1, T):
        total = total + stat1[k]
    total = over_groups(total, per_l) / count_l
    mean_l = total[0:1]
    inv_l = lax.rsqrt(total[1:2] - mean_l * mean_l + epsilon)
    v = (x - mean_l) * inv_l * gain_l[...] + shift_l[...]
    act[...] = (v * jax.nn.sigmoid(v)).astype(BF16).reshape(Fl, Rl, Cl, CH)
    lane = pl.multiple_of(lax.rem(h * CH, U), CH)
    mine = abuf.at[(h * CH) // U, pl.ds(2 + t * Fl, Fl), pl.ds(1, Rl), :, pl.ds(lane, CH)]
    a_in = [go(act, mine, at(kt, kh)) for kt, kh in peers]
    own_a = pltpu.make_async_copy(act, mine, local_sem.at[0])
    own_a.start()

    up_rows = CH // T
    up_cols = pl.ds(pl.multiple_of(half * (4 * C2), C2), 4 * C2)

    def up_piece(gt, gh):
        return upw.at[pl.ds(pl.multiple_of(gh * CH + gt * up_rows, up_rows), up_rows), up_cols]

    own_rows = up_w.at[pl.ds(pl.multiple_of(t * up_rows, up_rows), up_rows), up_cols]
    up_z = [go(own_rows, up_piece(t, h), at(0, kh)) for kh in range(1, H)]
    own_up = pltpu.make_async_copy(up_w, upw.at[pl.ds(pl.multiple_of(h * CH, CH), CH)], local_sem.at[1])
    own_up.start()

    def halo(buffer, frames_at, step, edge_src):
        made = []
        f_all, f_two, two_at, all_at = frames_at
        ok_t_send = (t < T - 1) if step == 1 else (t > 0)
        ok_t_recv = (t > 0) if step == 1 else (t < T - 1)
        kt = step % T
        for kt_, kh_, ok_s, ok_r, src, dst in (
            (kt, 0, ok_t_send, ok_t_recv, edge_src(f_two, 0, R), buffer.at[pl.ds(two_at, 2), pl.ds(1, R)]),
            (0, 1, h < H - 1, h > 0, edge_src(f_all, R - 1, 1), buffer.at[pl.ds(all_at, F), pl.ds(0, 1)]),
            (0, H - 1, h > 0, h < H - 1, edge_src(f_all, 0, 1), buffer.at[pl.ds(all_at, F), pl.ds(R + 1, 1)]),
            (kt, 1, ok_t_send & (h < H - 1), ok_t_recv & (h > 0),
             edge_src(f_two, R - 1, 1), buffer.at[pl.ds(two_at, 2), pl.ds(0, 1)]),
            (kt, H - 1, ok_t_send & (h > 0), ok_t_recv & (h < H - 1),
             edge_src(f_two, 0, 1), buffer.at[pl.ds(two_at, 2), pl.ds(R + 1, 1)]),
        ):
            c = copy(src, dst, at(kt_, kh_))
            pl.when(ok_s)(c.start)
            made.append((c, ok_s, ok_r))
        return made

    cot_halo = halo(
        cb, ((0, F), (0, 2), F, 0), -1,
        lambda fs, r0, n: cot.at[pl.ds(fs[0], fs[1]), pl.ds(r0, n)],
    )

    shard = w_b.shape[0]
    w_cols = pl.ds(pl.multiple_of(half * (C2 // 2), C2 // 2), C2 // 2)

    def w_piece(gt, gh):
        return wb.at[pl.ds(pl.multiple_of((gt * H + gh) * shard, shard), shard), w_cols]

    w_z = [go(w_b.at[:, w_cols], w_piece(t, h), at(0, 1))]
    w_y = [(kt, 0, go(w_b.at[:, w_cols], w_piece(t, h), at(kt, 0))) for kt in range(1, T)]
    own_w = pltpu.make_async_copy(
        w_b, wb.at[pl.ds(pl.multiple_of((t * H + h) * shard, shard), shard)], local_sem.at[2]
    )
    own_w.start()

    acc_l[...] = jnp.zeros(acc_l.shape, F32)
    own_a.wait()
    for made in a_in:
        made.wait_recv()
    cells_l = FL * Rl * Cl

    def latent_tap(j, _):
        unit = t * 27 + j
        tap, chunk = unit // T, unit % T
        lag, dr, dc = tap // 9, (tap // 3) % 3, tap % 3
        win = abuf[chunk, pl.ds(lag, FL), pl.ds(dr, Rl)].reshape(cells_l, U)
        rows = w_l[pl.ds(pl.multiple_of(j * U, U), U), :]
        acc_l[dc] += jnp.dot(win, rows, preferred_element_type=F32)
        return 0

    lax.fori_loop(0, 27, latent_tap, 0)
    mixed = column_shift(acc_l[0], Cl, 1) + acc_l[1] + column_shift(acc_l[2], Cl, -1)
    part[...] = mixed.reshape(FL, Rl, Cl, CH)
    part[pl.ds(t * Fl, Fl)] += latent[...].astype(F32)
    p_in = []
    for kt, kh in peers:
        dev = at(kt, kh)
        p_in.append(
            go(part.at[pl.ds(dev[1] * Fl, Fl), pl.ds(dev[2] * band, band)],
               parts_in.at[kt * H + kh], dev)
        )

    up_pair, up_y = [], []
    for kh in range(1, H):
        up_z[kh - 1].wait_recv()
        got = up_piece(t, lax.rem(h + H - kh, H))
        up_pair.append(go(got, got, (pair, t, h)))
        for kt in range(1, T):
            up_y.append((kt, kh, go(got, got, at(kt, 0))))

    w_z += [go(w_b.at[:, w_cols], w_piece(t, h), at(0, kh)) for kh in range(2, H)]

    for kt, kh, made in up_y:
        made.wait_recv()
        got = up_piece(lax.rem(t + T - kt, T), lax.rem(h + H - kh, H))
        up_pair.append(go(got, got, (pair, t, h)))
    for made in p_in:
        made.wait_recv()
    w_pair = []

    def w_onward(kh):
        w_z[kh - 1].wait_recv()
        got = w_piece(t, lax.rem(h + H - kh, H))
        w_pair.append(go(got, got, (pair, t, h)))
        for kt in range(1, T):
            w_y.append((kt, kh, go(got, got, at(kt, 0))))

    w_onward(1)
    own_up.wait()
    for made in up_pair:
        made.wait_recv()

    cells_b = Fl * band * Cl
    parts_own = part[pl.ds(t * Fl, Fl), pl.ds(h * band, band)]
    expanded = jnp.zeros((cells_b, 8 * C2), F32)
    for kh in range(H):
        value = parts_own if kh == 0 else parts_in[kh]
        for kt in range(1, T):
            value = value + parts_in[kt * H + kh]
        refined = value.reshape(cells_b, CH).astype(BF16)
        source = lax.rem(h + H - kh, H)
        expanded = expanded + jnp.dot(
            refined, upw[pl.ds(pl.multiple_of(source * CH, CH), CH), :],
            preferred_element_type=F32,
        )
    expanded = expanded.astype(BF16).astype(F32)
    for f in range(Fl):
        for r in range(band):
            for p in range(2):
                for q in range(2):
                    for s in range(2):
                        first = (f * band + r) * Cl
                        col = ((p * 2 + q) * 2 + s) * C2
                        for n in range(C2 // 128):
                            lace[
                                n, pl.ds(((2 * f + p) * R + 2 * r + q) * C + s, Cl, stride=2), :
                            ] = expanded[first : first + Cl, col + n * 128 : col + (n + 1) * 128]

    cells = F * R * C
    me = t * H + h
    up = jnp.concatenate([lace[n] for n in range(C2 // 128)], axis=1)
    upf[...] = up
    stat2[me] = two_rows(jnp.sum(up, 0, keepdims=True), jnp.sum(up * up, 0, keepdims=True))
    s2 = [go(stat2.at[me], stat2.at[me], at(kt, kh)) for kt, kh in peers]
    for made in s2:
        made.wait_recv()
    per_b = C2 // GROUPS
    count_b = cells * per_b * N
    total = stat2[0]
    for k in range(1, N):
        total = total + stat2[k]
    total = over_groups(total, per_b) / count_b
    mean_b = total[0:1]
    inv_b = lax.rsqrt(total[1:2] - mean_b * mean_b + epsilon)
    standard = (up - mean_b) * inv_b
    std[...] = standard
    normed = standard * gain_b[...] + shift_b[...]
    ab[2 : 2 + F, 1 : 1 + R] = (
        (normed * jax.nn.sigmoid(normed)).astype(BF16).reshape(F, R, C, C2)
    )
    ab_halo = halo(
        ab, ((2, F), (F, 2), 0, 2), 1,
        lambda fs, r0, n: ab.at[pl.ds(fs[0], fs[1]), pl.ds(1 + r0, n)],
    )

    for kh in range(2, H):
        w_onward(kh)

    for made, _, ok in ab_halo:
        pl.when(ok)(made.wait_recv)

    for dr in range(3):
        win = ab[2 : 2 + F, dr : dr + R].reshape(cells, C2)
        for dc in range(3):
            term = lax.dot_general(
                win, cot3[:, dc * C2 : (dc + 1) * C2],
                (((0,), (0,)), ((), ())), preferred_element_type=F32,
            )
            gw[(dr * 3 + dc) * C2 : (dr * 3 + dc + 1) * C2, :] = term.astype(BF16)
    out_rows = 9 * C2 // N
    y_rows = out_rows * H
    g_y = []
    for kt in range(1, T):
        dev = at(kt, 0)
        g_y.append(go(gw.at[pl.ds(pl.multiple_of(dev[1] * y_rows, y_rows), y_rows)], gy.at[kt], dev))

    for kt, kh, made in w_y:
        made.wait_recv()
        got = w_piece(lax.rem(t + T - kt, T), lax.rem(h + H - kh, H))
        w_pair.append(go(got, got, (pair, t, h)))
    for made, _, ok in cot_halo:
        pl.when(ok)(made.wait_recv)
    own_w.wait()
    for made in w_pair:
        made.wait_recv()

    acc[...] = jnp.zeros(acc.shape, F32)

    def grad_tap(j, _):
        lag, dr = j // 3, j % 3
        win = cb[pl.ds(2 - lag, F), pl.ds(2 - dr, R)].reshape(cells, C2)
        for dc in range(3):
            rows = wb[pl.ds(pl.multiple_of((j * 3 + dc) * C2, C2), C2), :]
            acc[dc] += lax.dot_general(
                win, rows, (((1,), (1,)), ((), ())), preferred_element_type=F32
            )
        return 0

    lax.fori_loop(0, 9, grad_tap, 0)
    grad_active = column_shift(acc[0], C, -1) + acc[1] + column_shift(acc[2], C, 1)
    standard = std[...]
    normed = standard * gain_b[...] + shift_b[...]
    sigmoid = jax.nn.sigmoid(normed)
    grad_normed = grad_active * sigmoid * (1.0 + normed * (1.0 - sigmoid))
    stat3[me] = two_rows(
        jnp.sum(grad_normed * standard, 0, keepdims=True), jnp.sum(grad_normed, 0, keepdims=True)
    )
    s3 = [go(stat3.at[me], stat3.at[me], at(kt, kh)) for kt, kh in peers]
    for made in g_y:
        made.wait_recv()
    summed = gw[pl.ds(pl.multiple_of(t * y_rows, y_rows), y_rows), :].astype(F32)
    for kt in range(1, T):
        summed = summed + gy[kt].astype(F32)
    gs[...] = summed.astype(BF16)
    g_z = []
    for kh in range(1, H):
        dev = at(0, kh)
        g_z.append(go(gs.at[pl.ds(pl.multiple_of(dev[2] * out_rows, out_rows), out_rows)], gz.at[kh], dev))

    upf_keep = upf[...]
    upf[...] = grad_normed * gain_b[...]

    acc[...] = jnp.zeros(acc.shape, F32)

    def tap(j, _):
        lag, dr = j // 3, j % 3
        win = ab[pl.ds(lag, F), pl.ds(dr, R)].reshape(cells, C2)
        for dc in range(3):
            rows = wb[pl.ds(pl.multiple_of((j * 3 + dc) * C2, C2), C2), :]
            acc[dc] += jnp.dot(win, rows, preferred_element_type=F32)
        return 0

    acc[1] = upf_keep
    lax.fori_loop(0, 9, tap, 0)
    decoded[...] = (
        (column_shift(acc[0], C, 1) + acc[1] + column_shift(acc[2], C, -1))
        .astype(BF16).reshape(F, R, C, C2)
    )

    for made in s3:
        made.wait_recv()
    total = stat3[0]
    for k in range(1, N):
        total = total + stat3[k]
    grad_gs[...] = total
    means = over_groups(total * gain_b[...], per_b) / count_b
    corrected = (upf[...] - means[1:2] - std[...] * means[0:1]) * inv_b
    grad_up[...] = (
        cot[...].astype(F32).reshape(cells, C2) + corrected
    ).astype(BF16).reshape(F, R, C, C2)

    for made in g_z:
        made.wait_recv()
    result = gs[pl.ds(pl.multiple_of(h * out_rows, out_rows), out_rows), :].astype(F32)
    for kh in range(1, H):
        result = result + gz[kh].astype(F32)
    grad_w[...] = result

    for made in sent:
        made.wait_send()
    for made, ok, _ in cot_halo + ab_halo:
        pl.when(ok)(made.wait_send)
    assert used[0] <= n_send


def local_block(shape, *args):
    (latent, gain_l, shift_l, w_l, up_w, gain_b, shift_b, w_b, cot) = args
    T, H = shape["tm"], shape["height"]
    Fl, Rl, Cl, CH = latent.shape
    F, R, C, C2 = cot.shape
    N = T * H
    U = H * CH // T
    fits = (
        shape["dp"] % 2 == 0
        and CH % 128 == 0 and U % CH == 0
        and w_b.shape[0] % 16 == 0 and (CH // T) % 16 == 0
        and (9 * C2) % (16 * N) == 0 and C2 % 256 == 0
        and Cl % 16 == 0 and w_l.shape[0] == 27 * U and F >= 2
    )
    if not fits:
        return local(*args)
    sizes = (T, H, Fl, Rl, Cl, CH, C2, F, R, C)
    n_send = 16 + 4 * T + 4 * N + 6 * N + 3 * N
    FL = T * Fl
    band = Rl // H
    cells = F * R * C
    out_rows = 9 * C2 // N
    vmem = pl.BlockSpec(memory_space=pltpu.VMEM)
    flops = 2 * (FL * Rl * Cl * w_l.size + 2 * cells * 27 * C2 * C2 + cells * 9 * C2 * C2)
    outs = pl.pallas_call(
        functools.partial(block_kernel, sizes, n_send),
        out_shape=(
            jax.ShapeDtypeStruct(cot.shape, BF16),
            jax.ShapeDtypeStruct(cot.shape, BF16),
            jax.ShapeDtypeStruct((out_rows, C2), F32),
            jax.ShapeDtypeStruct((8, C2), F32),
        ),
        in_specs=[vmem] * 9,
        out_specs=(vmem,) * 4,
        scratch_shapes=[
            pltpu.VMEM((Fl, Rl, Cl, CH), BF16),
            pltpu.VMEM((T, FL + 2, Rl + 2, Cl, U), BF16),
            pltpu.VMEM((3, FL * Rl * Cl, CH), F32),
            pltpu.VMEM((FL, Rl, Cl, CH), F32),
            pltpu.VMEM((N, Fl, band, Cl, CH), F32),
            pltpu.VMEM((T, 8, CH), F32),
            pltpu.VMEM((N, 8, C2), F32),
            pltpu.VMEM((N, 8, C2), F32),
            pltpu.VMEM((H * CH, 8 * C2), BF16),
            pltpu.VMEM((27 * C2, C2), BF16),
            pltpu.VMEM((cells, C2), F32),
            pltpu.VMEM((cells, C2), F32),
            pltpu.VMEM((F + 2, R + 2, C, C2), BF16),
            pltpu.VMEM((F + 2, R + 2, C, C2), BF16),
            pltpu.VMEM((cells, 3 * C2), BF16),
            pltpu.VMEM((9 * C2, C2), BF16),
            pltpu.VMEM((T, out_rows * H, C2), BF16),
            pltpu.VMEM((out_rows * H, C2), BF16),
            pltpu.VMEM((H, out_rows, C2), BF16),
            pltpu.VMEM((3, cells, C2), F32),
            pltpu.VMEM((C2 // 128, cells, 128), F32),
            pltpu.SemaphoreType.DMA((n_send,)),
            pltpu.SemaphoreType.DMA((n_send,)),
            pltpu.SemaphoreType.DMA((3,)),
        ],
        compiler_params=pltpu.CompilerParams(
            collective_id=0, has_side_effects=True, vmem_limit_bytes=60 * 1024 * 1024
        ),
        cost_estimate=pl.CostEstimate(flops=flops, bytes_accessed=1 << 23, transcendentals=0),
    )(
        latent, gain_l.reshape(1, -1), shift_l.reshape(1, -1), w_l, up_w,
        gain_b.reshape(1, -1), shift_b.reshape(1, -1), w_b, cot,
    )
    decoded, grad_up, grad_w, grad_gs = outs
    return decoded, grad_up, grad_w, grad_gs[0], grad_gs[1]


def solution(mesh):
    return jax.shard_map(
        functools.partial(local_block, dict(mesh.shape)),
        mesh=mesh,
        in_specs=(
            P(("dp", "tm"), None, None, "height"),
            P("height"),
            P("height"),
            P("tm", "height"),
            P("height", None),
            P(),
            P(),
            P(("tm", "height"), None),
            P(("dp", "tm"), "height", None, None),
        ),
        out_specs=(
            P(("dp", "tm"), "height", None, None),
            P(("dp", "tm"), "height", None, None),
            P(("dp", "tm", "height"), None),
            P("dp"),
            P("dp"),
        ),
        check_vma=False,
    )
```

profile of v0, /device:TPU:12, one launch (start us, length us, event | category | flops | bytes accessed | tf_op | source)
XLA Modules:
  0.0 110.7 jit_solution(379791696495080497)
XLA Ops:
  0.6 103.7 %shard_map.128 = (bf16[4,4,32,256]{3,2,1,0:T(8,128)(2,1)}, bf16[4,4,32,256]{3,2,1,0:T(8,128)(2,1)}, f32[288,256]{1,0:T(8,128)}, f32[8,256]{1,0:T(8,128)}) custom-call(bf16[2,8,16,128]{3,2,1,0:T(8,128)(2,1)} %refs_0_.1, f32[1,128]{1,0:T(1,128)} %bitcast.10, f32[1,128]{1,0:T(1,128)} %bitcast.11, bf16[6912,128]{1,0:T(8,128)(2,1)} %refs_3_.1, ...), custom_call_target="tpu_custom_call" | custom-call | flops 5133828096 | bytes 8388608 | tf_op jit(solution)/shard_map/pallas_call | solution.py:604
  104.3 1.3 %fusion = (f32[1,256]{1,0:T(1,128)}, f32[1,256]{1,0:T(1,128)}) fusion(f32[8,256]{1,0:T(8,128)} %get-tuple-element.12), kind=kLoop, calls=%fused_computation | loop fusion | bytes 4096 | tf_op jit(solution)/shard_map/slice | solution.py:649
  105.7 1.7 %copy.17 = bf16[4,4,32,256]{3,2,1,0:T(8,128)(2,1)} copy(bf16[4,4,32,256]{3,2,1,0:T(8,128)(2,1)} %get-tuple-element.20) | data formatting | bytes 524288
  107.3 1.7 %copy.18 = bf16[4,4,32,256]{3,2,1,0:T(8,128)(2,1)} copy(bf16[4,4,32,256]{3,2,1,0:T(8,128)(2,1)} %get-tuple-element.21) | data formatting | bytes 524288
  109.0 1.7 %copy.19 = f32[288,256]{1,0:T(8,128)} copy(f32[288,256]{1,0:T(8,128)} %get-tuple-element.22) | data formatting | bytes 589824
where the time goes:
time: 111 us
  Pallas kernels  104 us (94%)
  local copies, waits for them, and re-layouts  6.37 us (6%)
    pallas_call x1, Pallas kernels, local_block(): pl.pallas_call(functools.partial(block_kernel, sizes, n_send), out_shape=...  104 us
    unnamed x3, local copies, waits for them, and re-layouts  5.03 us

commit v1 on v0

--- a/solution.py
+++ b/solution.py
@@ -240,16 +240,18 @@
     (
         latent, gain_l, shift_l, w_l, up_w, gain_b, shift_b, w_b, cot,
         decoded, grad_up, grad_w, grad_gs,
-        act, abuf, acc_l, part, parts_in, stat1, stat2, stat3, upw, wb,
-        upf, std, ab, cb, cot3, gw, gy, gs, gz, acc, lace, send_sem, recv_sem, local_sem,
+        lbuf, gall, sall, wl, abuf, part, partf, parts_in, stat2, stat3, upw, wb,
+        ub, std, ab, cb, cot3, gw, gy, gs, gz, acc, tmp, lace, send_sem, recv_sem, local_sem,
     ) = refs
     d, t, h = lax.axis_index("dp"), lax.axis_index("tm"), lax.axis_index("height")
     N = T * H
     FL = T * Fl
     U = H * CH // T
     band = Rl // H
-    pair = d + 1 - 2 * (d % 2)
-    half = d % 2
+    q = lax.rem(d, 4)
+    half, side = lax.rem(q, 2), q // 2
+    pair = d + 1 - 2 * half
+    across = d + 2 - 4 * side
     used = [0]
     sent = []
 
@@ -270,184 +272,246 @@
         sent.append(made)
         return made
 
+    def scope(name):
+        return jax.named_scope(name)
+
+    def recv(name, *made):
+        with scope(name):
+            for m in made:
+                m.wait_recv()
+
     peers = [(kt, kh) for kt in range(T) for kh in range(H) if kt or kh]
-
-    abuf[...] = jnp.zeros(abuf.shape, BF16)
-    ab[...] = jnp.zeros(ab.shape, BF16)
+    far = [kh for kh in range(H // 2, H)] + [kh for kh in range(1, H // 2)]
+    shard = w_b.shape[0]
+
+    def local_copy(k, src, dst):
+        made = pltpu.make_async_copy(src, dst, local_sem.at[k])
+        made.start()
+        return made
+
+    own_l = local_copy(0, latent, lbuf.at[t, h])
     cb[...] = jnp.zeros(cb.shape, BF16)
-
     barrier = pltpu.get_barrier_semaphore()
     for kt, kh in peers:
         pl.semaphore_signal(barrier, inc=1, device_id=at(kt, kh), device_id_type=MESH)
     pl.semaphore_signal(barrier, inc=1, device_id=(pair, t, h), device_id_type=MESH)
-    pl.semaphore_wait(barrier, N)
-
-    x = latent[...].astype(F32).reshape(Fl * Rl * Cl, CH)
-    stat1[t] = two_rows(jnp.sum(x, 0, keepdims=True), jnp.sum(x * x, 0, keepdims=True))
-    s1 = [go(stat1.at[t], stat1.at[t], at(kt, 0)) for kt in range(1, T)]
-    cb[0:F, 1 : 1 + R] = cot[...]
-    wide = cot[...].astype(F32).reshape(F * R * C, C2)
-    cot3[:, 0:C2] = column_shift(wide, C, -1).astype(BF16)
-    cot3[:, C2 : 2 * C2] = cot[...].reshape(F * R * C, C2)
-    cot3[:, 2 * C2 :] = column_shift(wide, C, 1).astype(BF16)
-    for made in s1:
-        made.wait_recv()
+    pl.semaphore_signal(barrier, inc=1, device_id=(across, t, h), device_id_type=MESH)
+    own_up = local_copy(1, up_w, upw.at[pl.ds(pl.multiple_of(h * CH, CH), CH)])
+    own_w = local_copy(2, w_b, wb.at[pl.ds(pl.multiple_of((t * H + h) * shard, shard), shard)])
+    own_wl = local_copy(3, w_l, wl)
+    abuf[...] = jnp.zeros(abuf.shape, BF16)
+    ab[...] = jnp.zeros(ab.shape, BF16)
+    own_c = local_copy(4, cot, cb.at[pl.ds(0, F), pl.ds(1, R)])
+    gall[h] = gain_l[...]
+    sall[h] = shift_l[...]
+    own_l.wait()
+    with scope("w_barrier"):
+        pl.semaphore_wait(barrier, N + 1)
+
+    mine = lbuf.at[t, h]
+    lz = {kh: go(mine, mine, at(0, kh)) for kh in far}
+    gz_in = [go(gain_l, gall.at[h], at(0, kh)) for kh in range(1, H)]
+    gz_in += [go(shift_l, sall.at[h], at(0, kh)) for kh in range(1, H)]
+    ly = [go(mine, mine, at(kt, 0)) for kt in range(1, T)]
+
+    up_rows, up_cols = CH // T, 8 * C2 // 4
+
+    def up_piece(gt, gh, quarter):
+        return upw.at[
+            pl.ds(pl.multiple_of(gh * CH + gt * up_rows, up_rows), up_rows),
+            pl.ds(pl.multiple_of(quarter * up_cols, up_cols), up_cols),
+        ]
+
+    own_up.wait()
+    uz = {kh: go(up_piece(t, h, q), up_piece(t, h, q), at(0, kh)) for kh in far}
+
+    def back(kh):
+        return lax.rem(h + H - kh, H)
+
+    for kh in range(1, H):
+        recv("w_lz", lz[kh])
+        got = lbuf.at[t, back(kh)]
+        for kt in range(1, T):
+            ly.append(go(got, got, at(kt, 0)))
+
+    ux, upair, uy = [], [], []
+
+    def up_on(gt, gh):
+        piece = up_piece(gt, gh, q)
+        ux.append((gt, gh, go(piece, piece, (across, t, h))))
+        upair.append(go(piece, piece, (pair, t, h)))
+
+    for kh in range(1, H):
+        recv("w_uz", uz[kh])
+        piece = up_piece(t, back(kh), q)
+        for kt in range(1, T):
+            uy.append((kt, kh, go(piece, piece, at(kt, 0))))
+        up_on(t, back(kh))
+
+    recv("w_ly", *ly)
+    recv("w_gain", *gz_in)
+
     per_l = H * CH // GROUPS
-    count_l = FL * Rl * Cl * per_l
-    total = stat1[0]
-    for k in range(1, T):
-        total = total + stat1[k]
-    total = over_groups(total, per_l) / count_l
-    mean_l = total[0:1]
-    inv_l = lax.rsqrt(total[1:2] - mean_l * mean_l + epsilon)
-    v = (x - mean_l) * inv_l * gain_l[...] + shift_l[...]
-    act[...] = (v * jax.nn.sigmoid(v)).astype(BF16).reshape(Fl, Rl, Cl, CH)
-    lane = pl.multiple_of(lax.rem(h * CH, U), CH)
-    mine = abuf.at[(h * CH) // U, pl.ds(2 + t * Fl, Fl), pl.ds(1, Rl), :, pl.ds(lane, CH)]
-    a_in = [go(act, mine, at(kt, kh)) for kt, kh in peers]
-    own_a = pltpu.make_async_copy(act, mine, local_sem.at[0])
-    own_a.start()
-
-    up_rows = CH // T
-    up_cols = pl.ds(pl.multiple_of(half * (4 * C2), C2), 4 * C2)
-
-    def up_piece(gt, gh):
-        return upw.at[pl.ds(pl.multiple_of(gh * CH + gt * up_rows, up_rows), up_rows), up_cols]
-
-    own_rows = up_w.at[pl.ds(pl.multiple_of(t * up_rows, up_rows), up_rows), up_cols]
-    up_z = [go(own_rows, up_piece(t, h), at(0, kh)) for kh in range(1, H)]
-    own_up = pltpu.make_async_copy(up_w, upw.at[pl.ds(pl.multiple_of(h * CH, CH), CH)], local_sem.at[1])
-    own_up.start()
-
-    def halo(buffer, frames_at, step, edge_src):
+    cells_l = FL * Rl * Cl
+    count_l = cells_l * per_l
+    xs, rows = [], []
+    for k in range(H):
+        x = lbuf[:, k].astype(F32).reshape(cells_l, CH)
+        rows += [jnp.sum(x, 0, keepdims=True), jnp.sum(x * x, 0, keepdims=True)]
+    total = over_groups(jnp.concatenate(rows, 0), per_l) / count_l
+    for k in range(H):
+        mean = total[2 * k : 2 * k + 1]
+        inv = lax.rsqrt(total[2 * k + 1 : 2 * k + 2] - mean * mean + epsilon)
+        x = lbuf[:, k].astype(F32).reshape(cells_l, CH)
+        v = (x - mean) * inv * gall[k] + sall[k]
+        lane = k * CH % U
+        abuf[k * CH // U, 2 : 2 + FL, 1 : 1 + Rl, :, lane : lane + CH] = (
+            (v * jax.nn.sigmoid(v)).astype(BF16).reshape(FL, Rl, Cl, CH)
+        )
+
+    own_wl.wait()
+
+    def window(chunk, tap):
+        lag, dr = tap // 9, (tap // 3) % 3
+        return abuf[chunk, pl.ds(lag, FL), pl.ds(dr, Rl)].reshape(cells_l, U)
+
+    def w_rows(chunk, tap):
+        return wl[pl.ds(pl.multiple_of((tap * T + chunk - 27 * t) * U, U), U), :]
+
+    with scope("c_latent"):
+        sums = None
+        for g in range(4):
+            tap = jnp.where(t == 0, 3 * g, 15 + 3 * g)
+            for chunk in range(T):
+                k3 = jnp.concatenate([w_rows(chunk, tap + dc) for dc in range(3)], 1)
+                term = jnp.dot(window(chunk, tap), k3, preferred_element_type=F32)
+                sums = term if sums is None else sums + term
+        alone = jnp.where(t == 0, 12, 14)
+        k2 = jnp.concatenate([w_rows(t, alone), w_rows(t, 13)], 1)
+        both = jnp.dot(window(t, alone), k2, preferred_element_type=F32)
+        lone = both[:, :CH] + jnp.dot(
+            window(1 - t, alone), w_rows(1 - t, alone), preferred_element_type=F32
+        )
+        first = sums[:, :CH] + jnp.where(t == 0, lone, 0.0)
+        last = sums[:, 2 * CH :] + jnp.where(t == 0, 0.0, lone)
+        mixed = (
+            column_shift(first, Cl, 1) + sums[:, CH : 2 * CH] + both[:, CH:]
+            + column_shift(last, Cl, -1)
+        )
+        partf[...] = mixed.reshape(FL, Rl, Cl, CH)
+        partf[pl.ds(t * Fl, Fl)] += lbuf[t, h].astype(F32)
+        part[...] = partf[...].astype(BF16)
+    p_in = []
+    for kt, kh in [(kt, kh) for kh in far + [0] for kt in range(T) if kt or kh]:
+        dev = at(kt, kh)
+        p_in.append(
+            go(part.at[pl.ds(dev[1] * Fl, Fl), pl.ds(dev[2] * band, band)],
+               parts_in.at[kt * H + kh], dev)
+        )
+
+    own_w.wait()
+    own_c.wait()
+    w_half = shard // 2
+
+    def w_piece(gt, gh, piece_side):
+        start = pl.multiple_of((gt * H + gh) * shard + piece_side * w_half, w_half)
+        return wb.at[pl.ds(start, w_half), pl.ds(pl.multiple_of(half * (C2 // 2), C2 // 2), C2 // 2)]
+
+    w_mine = w_piece(t, h, side)
+    wz = {kh: go(w_mine, w_mine, at(0, kh)) for kh in far}
+    wy = [(kt, 0, go(w_mine, w_mine, at(kt, 0))) for kt in range(1, T)]
+    wx, wpair = [], []
+
+    def w_on(gt, gh):
+        piece = w_piece(gt, gh, side)
+        wx.append((gt, gh, go(piece, piece, (across, t, h))))
+        wpair.append(go(piece, piece, (pair, t, h)))
+
+    def halo(buffer, f0, f_two, two_at, step):
         made = []
-        f_all, f_two, two_at, all_at = frames_at
         ok_t_send = (t < T - 1) if step == 1 else (t > 0)
         ok_t_recv = (t > 0) if step == 1 else (t < T - 1)
         kt = step % T
+
+        def part_of(fs, n_f, r0, n_r):
+            return buffer.at[pl.ds(fs, n_f), pl.ds(r0, n_r)]
+
         for kt_, kh_, ok_s, ok_r, src, dst in (
-            (kt, 0, ok_t_send, ok_t_recv, edge_src(f_two, 0, R), buffer.at[pl.ds(two_at, 2), pl.ds(1, R)]),
-            (0, 1, h < H - 1, h > 0, edge_src(f_all, R - 1, 1), buffer.at[pl.ds(all_at, F), pl.ds(0, 1)]),
-            (0, H - 1, h > 0, h < H - 1, edge_src(f_all, 0, 1), buffer.at[pl.ds(all_at, F), pl.ds(R + 1, 1)]),
+            (kt, 0, ok_t_send, ok_t_recv, part_of(f_two, 2, 1, R), part_of(two_at, 2, 1, R)),
+            (0, 1, h < H - 1, h > 0, part_of(f0, F, R, 1), part_of(f0, F, 0, 1)),
+            (0, H - 1, h > 0, h < H - 1, part_of(f0, F, 1, 1), part_of(f0, F, R + 1, 1)),
             (kt, 1, ok_t_send & (h < H - 1), ok_t_recv & (h > 0),
-             edge_src(f_two, R - 1, 1), buffer.at[pl.ds(two_at, 2), pl.ds(0, 1)]),
+             part_of(f_two, 2, R, 1), part_of(two_at, 2, 0, 1)),
             (kt, H - 1, ok_t_send & (h > 0), ok_t_recv & (h < H - 1),
-             edge_src(f_two, 0, 1), buffer.at[pl.ds(two_at, 2), pl.ds(R + 1, 1)]),
+             part_of(f_two, 2, 1, 1), part_of(two_at, 2, R + 1, 1)),
         ):
             c = copy(src, dst, at(kt_, kh_))
             pl.when(ok_s)(c.start)
             made.append((c, ok_s, ok_r))
         return made
 
-    cot_halo = halo(
-        cb, ((0, F), (0, 2), F, 0), -1,
-        lambda fs, r0, n: cot.at[pl.ds(fs[0], fs[1]), pl.ds(r0, n)],
-    )
-
-    shard = w_b.shape[0]
-    w_cols = pl.ds(pl.multiple_of(half * (C2 // 2), C2 // 2), C2 // 2)
-
-    def w_piece(gt, gh):
-        return wb.at[pl.ds(pl.multiple_of((gt * H + gh) * shard, shard), shard), w_cols]
-
-    w_z = [go(w_b.at[:, w_cols], w_piece(t, h), at(0, 1))]
-    w_y = [(kt, 0, go(w_b.at[:, w_cols], w_piece(t, h), at(kt, 0))) for kt in range(1, T)]
-    own_w = pltpu.make_async_copy(
-        w_b, wb.at[pl.ds(pl.multiple_of((t * H + h) * shard, shard), shard)], local_sem.at[2]
-    )
-    own_w.start()
-
-    acc_l[...] = jnp.zeros(acc_l.shape, F32)
-    own_a.wait()
-    for made in a_in:
-        made.wait_recv()
-    cells_l = FL * Rl * Cl
-
-    def latent_tap(j, _):
-        unit = t * 27 + j
-        tap, chunk = unit // T, unit % T
-        lag, dr, dc = tap // 9, (tap // 3) % 3, tap % 3
-        win = abuf[chunk, pl.ds(lag, FL), pl.ds(dr, Rl)].reshape(cells_l, U)
-        rows = w_l[pl.ds(pl.multiple_of(j * U, U), U), :]
-        acc_l[dc] += jnp.dot(win, rows, preferred_element_type=F32)
-        return 0
-
-    lax.fori_loop(0, 27, latent_tap, 0)
-    mixed = column_shift(acc_l[0], Cl, 1) + acc_l[1] + column_shift(acc_l[2], Cl, -1)
-    part[...] = mixed.reshape(FL, Rl, Cl, CH)
-    part[pl.ds(t * Fl, Fl)] += latent[...].astype(F32)
-    p_in = []
-    for kt, kh in peers:
-        dev = at(kt, kh)
-        p_in.append(
-            go(part.at[pl.ds(dev[1] * Fl, Fl), pl.ds(dev[2] * band, band)],
-               parts_in.at[kt * H + kh], dev)
-        )
-
-    up_pair, up_y = [], []
+    cot_halo = halo(cb, 0, 0, F, -1)
+
+    for kt, kh, made in uy:
+        recv("w_uy", made)
+        up_on(lax.rem(t + T - kt, T), back(kh))
+    for gt, gh, made in ux:
+        recv("w_ux", made)
+        piece = up_piece(gt, gh, lax.rem(q + 2, 4))
+        upair.append(go(piece, piece, (pair, t, h)))
+    recv("w_upair", *upair)
+    recv("w_parts", *p_in)
+
+    cells_b = Fl * band * Cl
+    with scope("c_up"):
+        parts_own = partf[pl.ds(t * Fl, Fl), pl.ds(h * band, band)]
+        expanded = jnp.zeros((cells_b, 8 * C2), F32)
+        for kh in range(H):
+            value = parts_own if kh == 0 else parts_in[kh].astype(F32)
+            for kt in range(1, T):
+                value = value + parts_in[kt * H + kh].astype(F32)
+            refined = value.reshape(cells_b, CH).astype(BF16)
+            source = back(kh)
+            expanded = expanded + jnp.dot(
+                refined, upw[pl.ds(pl.multiple_of(source * CH, CH), CH), :],
+                preferred_element_type=F32,
+            )
+        expanded = expanded.astype(BF16).astype(F32)
+        for f in range(Fl):
+            for r in range(band):
+                for p in range(2):
+                    for qq in range(2):
+                        for s in range(2):
+                            first = (f * band + r) * Cl
+                            col = ((p * 2 + qq) * 2 + s) * C2
+                            for n in range(C2 // 128):
+                                lace[
+                                    n, pl.ds(((2 * f + p) * R + 2 * r + qq) * C + s, Cl, stride=2), :
+                                ] = expanded[first : first + Cl, col + n * 128 : col + (n + 1) * 128]
+
+        cells = F * R * C
+        me = t * H + h
+        up = jnp.concatenate([lace[n] for n in range(C2 // 128)], axis=1)
+        stat2[me] = two_rows(jnp.sum(up, 0, keepdims=True), jnp.sum(up * up, 0, keepdims=True))
+        ub[2 : 2 + F, 1 : 1 + R] = up.astype(BF16).reshape(F, R, C, C2)
+    s2 = [go(stat2.at[me], stat2.at[me], at(kt, kh)) for kt, kh in peers]
+    up_halo = halo(ub, 2, F, 0, 1)
+
     for kh in range(1, H):
-        up_z[kh - 1].wait_recv()
-        got = up_piece(t, lax.rem(h + H - kh, H))
-        up_pair.append(go(got, got, (pair, t, h)))
+        recv("w_wz", wz[kh])
+        piece = w_piece(t, back(kh), side)
         for kt in range(1, T):
-            up_y.append((kt, kh, go(got, got, at(kt, 0))))
-
-    w_z += [go(w_b.at[:, w_cols], w_piece(t, h), at(0, kh)) for kh in range(2, H)]
-
-    for kt, kh, made in up_y:
-        made.wait_recv()
-        got = up_piece(lax.rem(t + T - kt, T), lax.rem(h + H - kh, H))
-        up_pair.append(go(got, got, (pair, t, h)))
-    for made in p_in:
-        made.wait_recv()
-    w_pair = []
-
-    def w_onward(kh):
-        w_z[kh - 1].wait_recv()
-        got = w_piece(t, lax.rem(h + H - kh, H))
-        w_pair.append(go(got, got, (pair, t, h)))
-        for kt in range(1, T):
-            w_y.append((kt, kh, go(got, got, at(kt, 0))))
-
-    w_onward(1)
-    own_up.wait()
-    for made in up_pair:
-        made.wait_recv()
-
-    cells_b = Fl * band * Cl
-    parts_own = part[pl.ds(t * Fl, Fl), pl.ds(h * band, band)]
-    expanded = jnp.zeros((cells_b, 8 * C2), F32)
-    for kh in range(H):
-        value = parts_own if kh == 0 else parts_in[kh]
-        for kt in range(1, T):
-            value = value + parts_in[kt * H + kh]
-        refined = value.reshape(cells_b, CH).astype(BF16)
-        source = lax.rem(h + H - kh, H)
-        expanded = expanded + jnp.dot(
-            refined, upw[pl.ds(pl.multiple_of(source * CH, CH), CH), :],
-            preferred_element_type=F32,
-        )
-    expanded = expanded.astype(BF16).astype(F32)
-    for f in range(Fl):
-        for r in range(band):
-            for p in range(2):
-                for q in range(2):
-                    for s in range(2):
-                        first = (f * band + r) * Cl
-                        col = ((p * 2 + q) * 2 + s) * C2
-                        for n in range(C2 // 128):
-                            lace[
-                                n, pl.ds(((2 * f + p) * R + 2 * r + q) * C + s, Cl, stride=2), :
-                            ] = expanded[first : first + Cl, col + n * 128 : col + (n + 1) * 128]
-
-    cells = F * R * C
-    me = t * H + h
-    up = jnp.concatenate([lace[n] for n in range(C2 // 128)], axis=1)
-    upf[...] = up
-    stat2[me] = two_rows(jnp.sum(up, 0, keepdims=True), jnp.sum(up * up, 0, keepdims=True))
-    s2 = [go(stat2.at[me], stat2.at[me], at(kt, kh)) for kt, kh in peers]
-    for made in s2:
-        made.wait_recv()
+            wy.append((kt, kh, go(piece, piece, at(kt, 0))))
+        w_on(t, back(kh))
+    with scope("w_cothalo"):
+        for made, _, ok in cot_halo:
+            pl.when(ok)(made.wait_recv)
+    wide = cb[0:F].astype(F32).reshape(F * (R + 2) * C, C2)
+    cot3[:, :, :, 0:C2] = column_shift(wide, C, -1).astype(BF16).reshape(F, R + 2, C, C2)
+    cot3[:, :, :, C2 : 2 * C2] = cb[0:F]
+    cot3[:, :, :, 2 * C2 :] = column_shift(wide, C, 1).astype(BF16).reshape(F, R + 2, C, C2)
+
+    recv("w_s2", *s2)
     per_b = C2 // GROUPS
     count_b = cells * per_b * N
     total = stat2[0]
@@ -456,47 +520,81 @@
     total = over_groups(total, per_b) / count_b
     mean_b = total[0:1]
     inv_b = lax.rsqrt(total[1:2] - mean_b * mean_b + epsilon)
-    standard = (up - mean_b) * inv_b
-    std[...] = standard
-    normed = standard * gain_b[...] + shift_b[...]
-    ab[2 : 2 + F, 1 : 1 + R] = (
-        (normed * jax.nn.sigmoid(normed)).astype(BF16).reshape(F, R, C, C2)
-    )
-    ab_halo = halo(
-        ab, ((2, F), (F, 2), 0, 2), 1,
-        lambda fs, r0, n: ab.at[pl.ds(fs[0], fs[1]), pl.ds(1 + r0, n)],
-    )
-
-    for kh in range(2, H):
-        w_onward(kh)
-
-    for made, _, ok in ab_halo:
-        pl.when(ok)(made.wait_recv)
-
-    for dr in range(3):
-        win = ab[2 : 2 + F, dr : dr + R].reshape(cells, C2)
-        for dc in range(3):
+
+    def activate(values):
+        normed = (values - mean_b) * inv_b * gain_b[...] + shift_b[...]
+        return (normed * jax.nn.sigmoid(normed)).astype(BF16)
+
+    with scope("c_gw"):
+        own = activate(ub[2 : 2 + F, 1 : 1 + R].astype(F32).reshape(cells, C2))
+        ab[2 : 2 + F, 1 : 1 + R] = own.reshape(F, R, C, C2)
+        for dr in range(3):
             term = lax.dot_general(
-                win, cot3[:, dc * C2 : (dc + 1) * C2],
+                own, cot3[:, 2 - dr : 2 - dr + R].reshape(cells, 3 * C2),
                 (((0,), (0,)), ((), ())), preferred_element_type=F32,
             )
-            gw[(dr * 3 + dc) * C2 : (dr * 3 + dc + 1) * C2, :] = term.astype(BF16)
+            for dc in range(3):
+                gw[(dr * 3 + dc) * C2 : (dr * 3 + dc + 1) * C2, :] = (
+                    term[:, dc * C2 : (dc + 1) * C2].astype(BF16)
+                )
     out_rows = 9 * C2 // N
     y_rows = out_rows * H
+
+    def g_rows(gt, gh):
+        return gw.at[pl.ds(pl.multiple_of((gt * H + gh) * out_rows, out_rows), out_rows)]
+
+    def ahead(kh):
+        return lax.rem(h + kh, H)
+
     g_y = []
-    for kt in range(1, T):
-        dev = at(kt, 0)
-        g_y.append(go(gw.at[pl.ds(pl.multiple_of(dev[1] * y_rows, y_rows), y_rows)], gy.at[kt], dev))
-
-    for kt, kh, made in w_y:
-        made.wait_recv()
-        got = w_piece(lax.rem(t + T - kt, T), lax.rem(h + H - kh, H))
-        w_pair.append(go(got, got, (pair, t, h)))
-    for made, _, ok in cot_halo:
-        pl.when(ok)(made.wait_recv)
-    own_w.wait()
-    for made in w_pair:
-        made.wait_recv()
+    for kh in far + [0]:
+        for kt in range(1, T):
+            dev = at(kt, 0)
+            g_y.append((kh, kt, go(g_rows(dev[1], ahead(kh)), gy.at[kt, kh], dev)))
+
+    for kt, kh, made in wy:
+        recv("w_wy", made)
+        w_on(lax.rem(t + T - kt, T), back(kh))
+    with scope("w_uphalo"):
+        for made, _, ok in up_halo:
+            pl.when(ok)(made.wait_recv)
+    with scope("c_halo"):
+        for rows_at, n_rows, ok in ((0, 1, h > 0), (R + 1, 1, h < H - 1)):
+            @pl.when(ok)
+            def _():
+                v = ub[2 : 2 + F, rows_at : rows_at + n_rows].astype(F32).reshape(F * n_rows * C, C2)
+                ab[2 : 2 + F, rows_at : rows_at + n_rows] = activate(v).reshape(F, n_rows, C, C2)
+        for rows_at, n_rows, ok in (
+            (1, R, t > 0), (0, 1, (t > 0) & (h > 0)), (R + 1, 1, (t > 0) & (h < H - 1))
+        ):
+            @pl.when(ok)
+            def _():
+                v = ub[0:2, rows_at : rows_at + n_rows].astype(F32).reshape(2 * n_rows * C, C2)
+                ab[0:2, rows_at : rows_at + n_rows] = activate(v).reshape(2, n_rows, C, C2)
+
+    for gt, gh, made in wx:
+        recv("w_wx", made)
+        piece = w_piece(gt, gh, 1 - side)
+        wpair.append(go(piece, piece, (pair, t, h)))
+
+    g_z = {}
+
+    def g_on(kh):
+        total = None
+        for made_kh, kt, made in g_y:
+            if made_kh == kh:
+                recv("w_gy", made)
+                term = gy[kt, kh].astype(F32)
+                total = term if total is None else total + term
+        start = pl.multiple_of((t * H + ahead(kh)) * out_rows, out_rows)
+        total = total + gw[pl.ds(start, out_rows), :].astype(F32)
+        if kh == 0:
+            grad_w[...] = total
+        else:
+            gs[kh] = total.astype(BF16)
+            g_z[kh] = go(gs.at[kh], gz.at[kh], at(0, kh))
+
+    recv("w_wpair", *wpair)
 
     acc[...] = jnp.zeros(acc.shape, F32)
 
@@ -510,9 +608,11 @@
             )
         return 0
 
-    lax.fori_loop(0, 9, grad_tap, 0)
+    with scope("c_gradtap"):
+        lax.fori_loop(0, 9, grad_tap, 0)
     grad_active = column_shift(acc[0], C, -1) + acc[1] + column_shift(acc[2], C, 1)
-    standard = std[...]
+    standard = (ub[2 : 2 + F, 1 : 1 + R].astype(F32).reshape(cells, C2) - mean_b) * inv_b
+    std[...] = standard
     normed = standard * gain_b[...] + shift_b[...]
     sigmoid = jax.nn.sigmoid(normed)
     grad_normed = grad_active * sigmoid * (1.0 + normed * (1.0 - sigmoid))
@@ -520,21 +620,13 @@
         jnp.sum(grad_normed * standard, 0, keepdims=True), jnp.sum(grad_normed, 0, keepdims=True)
     )
     s3 = [go(stat3.at[me], stat3.at[me], at(kt, kh)) for kt, kh in peers]
-    for made in g_y:
-        made.wait_recv()
-    summed = gw[pl.ds(pl.multiple_of(t * y_rows, y_rows), y_rows), :].astype(F32)
-    for kt in range(1, T):
-        summed = summed + gy[kt].astype(F32)
-    gs[...] = summed.astype(BF16)
-    g_z = []
-    for kh in range(1, H):
-        dev = at(0, kh)
-        g_z.append(go(gs.at[pl.ds(pl.multiple_of(dev[2] * out_rows, out_rows), out_rows)], gz.at[kh], dev))
-
-    upf_keep = upf[...]
-    upf[...] = grad_normed * gain_b[...]
-
-    acc[...] = jnp.zeros(acc.shape, F32)
+    tmp[...] = grad_normed * gain_b[...]
+    for kh in far:
+        g_on(kh)
+
+    acc[0] = jnp.zeros((cells, C2), F32)
+    acc[1] = ub[2 : 2 + F, 1 : 1 + R].astype(F32).reshape(cells, C2)
+    acc[2] = jnp.zeros((cells, C2), F32)
 
     def tap(j, _):
         lag, dr = j // 3, j % 3
@@ -544,36 +636,36 @@
             acc[dc] += jnp.dot(win, rows, preferred_element_type=F32)
         return 0
 
-    acc[1] = upf_keep
-    lax.fori_loop(0, 9, tap, 0)
+    with scope("c_tap"):
+        lax.fori_loop(0, 9, tap, 0)
     decoded[...] = (
         (column_shift(acc[0], C, 1) + acc[1] + column_shift(acc[2], C, -1))
         .astype(BF16).reshape(F, R, C, C2)
     )
-
-    for made in s3:
-        made.wait_recv()
+    g_on(0)
+
+    recv("w_s3", *s3)
     total = stat3[0]
     for k in range(1, N):
         total = total + stat3[k]
     grad_gs[...] = total
     means = over_groups(total * gain_b[...], per_b) / count_b
-    corrected = (upf[...] - means[1:2] - std[...] * means[0:1]) * inv_b
+    corrected = (tmp[...] - means[1:2] - std[...] * means[0:1]) * inv_b
     grad_up[...] = (
-        cot[...].astype(F32).reshape(cells, C2) + corrected
+        cb[0:F, 1 : 1 + R].astype(F32).reshape(cells, C2) + corrected
     ).astype(BF16).reshape(F, R, C, C2)
 
-    for made in g_z:
-        made.wait_recv()
-    result = gs[pl.ds(pl.multiple_of(h * out_rows, out_rows), out_rows), :].astype(F32)
+    recv("w_gz", *g_z.values())
+    result = grad_w[...]
     for kh in range(1, H):
         result = result + gz[kh].astype(F32)
     grad_w[...] = result
 
-    for made in sent:
-        made.wait_send()
-    for made, ok, _ in cot_halo + ab_halo:
-        pl.when(ok)(made.wait_send)
+    with scope("w_send"):
+        for made in sent:
+            made.wait_send()
+        for made, ok, _ in cot_halo + up_halo:
+            pl.when(ok)(made.wait_send)
     assert used[0] <= n_send
 
 
@@ -585,21 +677,22 @@
     N = T * H
     U = H * CH // T
     fits = (
-        shape["dp"] % 2 == 0
+        shape["dp"] % 4 == 0 and T == 2
         and CH % 128 == 0 and U % CH == 0
-        and w_b.shape[0] % 16 == 0 and (CH // T) % 16 == 0
+        and w_b.shape[0] % 32 == 0 and (CH // T) % 16 == 0
         and (9 * C2) % (16 * N) == 0 and C2 % 256 == 0
         and Cl % 16 == 0 and w_l.shape[0] == 27 * U and F >= 2
     )
     if not fits:
         return local(*args)
     sizes = (T, H, Fl, Rl, Cl, CH, C2, F, R, C)
-    n_send = 16 + 4 * T + 4 * N + 6 * N + 3 * N
+    n_send = 200
     FL = T * Fl
     band = Rl // H
     cells = F * R * C
     out_rows = 9 * C2 // N
     vmem = pl.BlockSpec(memory_space=pltpu.VMEM)
+    hbm = pl.BlockSpec(memory_space=pl.ANY)
     flops = 2 * (FL * Rl * Cl * w_l.size + 2 * cells * 27 * C2 * C2 + cells * 9 * C2 * C2)
     outs = pl.pallas_call(
         functools.partial(block_kernel, sizes, n_send),
@@ -609,33 +702,36 @@
             jax.ShapeDtypeStruct((out_rows, C2), F32),
             jax.ShapeDtypeStruct((8, C2), F32),
         ),
-        in_specs=[vmem] * 9,
+        in_specs=[hbm, vmem, vmem, hbm, hbm, vmem, vmem, hbm, hbm],
         out_specs=(vmem,) * 4,
         scratch_shapes=[
-            pltpu.VMEM((Fl, Rl, Cl, CH), BF16),
+            pltpu.VMEM((T, H, Fl, Rl, Cl, CH), BF16),
+            pltpu.VMEM((H, 1, CH), F32),
+            pltpu.VMEM((H, 1, CH), F32),
+            pltpu.VMEM(w_l.shape, BF16),
             pltpu.VMEM((T, FL + 2, Rl + 2, Cl, U), BF16),
-            pltpu.VMEM((3, FL * Rl * Cl, CH), F32),
+            pltpu.VMEM((FL, Rl, Cl, CH), BF16),
             pltpu.VMEM((FL, Rl, Cl, CH), F32),
-            pltpu.VMEM((N, Fl, band, Cl, CH), F32),
-            pltpu.VMEM((T, 8, CH), F32),
+            pltpu.VMEM((N, Fl, band, Cl, CH), BF16),
             pltpu.VMEM((N, 8, C2), F32),
             pltpu.VMEM((N, 8, C2), F32),
             pltpu.VMEM((H * CH, 8 * C2), BF16),
             pltpu.VMEM((27 * C2, C2), BF16),
-            pltpu.VMEM((cells, C2), F32),
+            pltpu.VMEM((F + 2, R + 2, C, C2), BF16),
             pltpu.VMEM((cells, C2), F32),
             pltpu.VMEM((F + 2, R + 2, C, C2), BF16),
             pltpu.VMEM((F + 2, R + 2, C, C2), BF16),
-            pltpu.VMEM((cells, 3 * C2), BF16),
+            pltpu.VMEM((F, R + 2, C, 3 * C2), BF16),
             pltpu.VMEM((9 * C2, C2), BF16),
-            pltpu.VMEM((T, out_rows * H, C2), BF16),
-            pltpu.VMEM((out_rows * H, C2), BF16),
+            pltpu.VMEM((T, H, out_rows, C2), BF16),
+            pltpu.VMEM((H, out_rows, C2), BF16),
             pltpu.VMEM((H, out_rows, C2), BF16),
             pltpu.VMEM((3, cells, C2), F32),
+            pltpu.VMEM((cells, C2), F32),
             pltpu.VMEM((C2 // 128, cells, 128), F32),
             pltpu.SemaphoreType.DMA((n_send,)),
             pltpu.SemaphoreType.DMA((n_send,)),
-            pltpu.SemaphoreType.DMA((3,)),
+            pltpu.SemaphoreType.DMA((5,)),
         ],
         compiler_params=pltpu.CompilerParams(
             collective_id=0, has_side_effects=True, vmem_limit_bytes=60 * 1024 * 1024

time: 111 us -> 82.8 us (0.75)
  the two profiles are of different devices: /device:TPU:12 before, /device:TPU:0 now
where the time goes in v1:
time: 82.8 us; the launch traced here: 81.5 us
  Pallas kernels  74.5 us (90%)
  local copies, waits for them, and re-layouts  6.37 us (8%)
    pallas_call x1, Pallas kernels, local_block(): pl.pallas_call(functools.partial(block_kernel, sizes, n_send), out_shape=...  74.5 us
    unnamed x3, local copies, waits for them, and re-layouts  5.03 us

profile of v1, /device:TPU:0, one launch (start us, length us, event | category | flops | bytes accessed | tf_op | source)
XLA Modules:
  0.0 81.5 jit_solution(8574843944567415538)
XLA Ops:
  0.6 74.5 %shard_map.128 = (bf16[4,4,32,256]{3,2,1,0:T(8,128)(2,1)}, bf16[4,4,32,256]{3,2,1,0:T(8,128)(2,1)}, f32[288,256]{1,0:T(8,128)}, f32[8,256]{1,0:T(8,128)}) custom-call(bf16[2,8,16,128]{3,2,1,0:T(8,128)(2,1)} %refs_0_.1, f32[1,128]{1,0:T(1,128)} %bitcast.10, f32[1,128]{1,0:T(1,128)} %bitcast.11, bf16[6912,128]{1,0:T(8,128)(2,1)} %refs_3_.1, ...), custom_call_target="tpu_custom_call" | custom-call | flops 5133828096 | bytes 8388608 | tf_op jit(solution)/shard_map/pallas_call | solution.py:697
  75.1 1.3 %fusion = (f32[1,256]{1,0:T(1,128)}, f32[1,256]{1,0:T(1,128)}) fusion(f32[8,256]{1,0:T(8,128)} %get-tuple-element.12), kind=kLoop, calls=%fused_computation | loop fusion | bytes 4096 | tf_op jit(solution)/shard_map/slice | solution.py:745
  76.5 1.7 %copy.17 = bf16[4,4,32,256]{3,2,1,0:T(8,128)(2,1)} copy(bf16[4,4,32,256]{3,2,1,0:T(8,128)(2,1)} %get-tuple-element.20) | data formatting | bytes 524288
  78.1 1.7 %copy.18 = bf16[4,4,32,256]{3,2,1,0:T(8,128)(2,1)} copy(bf16[4,4,32,256]{3,2,1,0:T(8,128)(2,1)} %get-tuple-element.21) | data formatting | bytes 524288
  79.8 1.7 %copy.19 = f32[288,256]{1,0:T(8,128)} copy(f32[288,256]{1,0:T(8,128)} %get-tuple-element.22) | data formatting | bytes 589824

commit v2 on v1

--- a/solution.py
+++ b/solution.py
@@ -203,6 +203,8 @@
 
 
 MESH = pl.DeviceIdType.MESH
+VMEM_LIMIT = 32 * 1024 * 1024
+W_EARLY = 2
 F32 = jnp.float32
 BF16 = jnp.bfloat16
 
@@ -235,13 +237,13 @@
     return jnp.where(row == 0, first, jnp.where(row == 1, second, 0.0))
 
 
-def block_kernel(sizes, n_send, *refs):
+def block_kernel(sizes, n_send, n_recv, *refs):
     (T, H, Fl, Rl, Cl, CH, C2, F, R, C) = sizes
     (
-        latent, gain_l, shift_l, w_l, up_w, gain_b, shift_b, w_b, cot,
+        latent, gain_in, shift_in, w_l, up_w, gain_b_in, shift_b_in, w_b, cot,
         decoded, grad_up, grad_w, grad_gs,
-        lbuf, gall, sall, wl, abuf, part, partf, parts_in, stat2, stat3, upw, wb,
-        ub, std, ab, cb, cot3, gw, gy, gs, gz, acc, tmp, lace, send_sem, recv_sem, local_sem,
+        lbuf, gall, gain_b, shift_b, wl, abuf, part, partf, parts_in, stat2, stat3, upw, wb,
+        ub, std, ab, cb, cot3, gw, gy, gs, gz, tmp, lace, send_sem, recv_sem, local_sem,
     ) = refs
     d, t, h = lax.axis_index("dp"), lax.axis_index("tm"), lax.axis_index("height")
     N = T * H
@@ -252,104 +254,197 @@
     half, side = lax.rem(q, 2), q // 2
     pair = d + 1 - 2 * half
     across = d + 2 - 4 * side
-    used = [0]
-    sent = []
+    counts = [0, 0]
+
+    def new_send():
+        counts[0] += 1
+        return send_sem.at[counts[0] - 1]
+
+    def new_recv(n=1):
+        counts[1] += n
+        return recv_sem.at[counts[1] - 1] if n == 1 else counts[1] - n
 
     def at(kt, kh):
         return (d, lax.rem(t + kt, T), lax.rem(h + kh, H))
 
-    def copy(src, dst, device):
-        k = used[0]
-        used[0] += 1
+    def copy(src, dst, device, s_sem, r_sem):
         return pltpu.make_async_remote_copy(
-            src_ref=src, dst_ref=dst, send_sem=send_sem.at[k], recv_sem=recv_sem.at[k],
+            src_ref=src, dst_ref=dst, send_sem=s_sem, recv_sem=r_sem,
             device_id=device, device_id_type=MESH,
         )
 
-    def go(src, dst, device):
-        made = copy(src, dst, device)
-        made.start()
-        sent.append(made)
-        return made
+    def go(*what):
+        copy(*what).start()
+
+    pair_dev, across_dev = (pair, t, h), (across, t, h)
+    left = []
+
+    def got(name, ref, r_sem):
+        with scope(name):
+            copy(ref, ref, pair_dev, send_sem.at[0], r_sem).wait_recv()
+
+    def left_all(ref, s_sem):
+        left.append((ref, s_sem))
 
     def scope(name):
         return jax.named_scope(name)
 
-    def recv(name, *made):
-        with scope(name):
-            for m in made:
-                m.wait_recv()
-
-    peers = [(kt, kh) for kt in range(T) for kh in range(H) if kt or kh]
-    far = [kh for kh in range(H // 2, H)] + [kh for kh in range(1, H // 2)]
+    peers = [(kt, kh) for kh in [*range(H // 2, H), *range(1, H // 2), 0] for kt in range(T) if kt or kh]
     shard = w_b.shape[0]
 
     def local_copy(k, src, dst):
         made = pltpu.make_async_copy(src, dst, local_sem.at[k])
         made.start()
         return made
+
+    def near(i):
+        where = 0
+        for hh in range(H):
+            order = sorted((o for o in range(H) if o != hh), key=lambda o: (abs(o - hh), -o))
+            where = where + jnp.where(h == hh, order[i], 0)
+        return where
+
+    nearest = [near(i) for i in range(H - 1)]
+
+    class Along:
+        def __init__(self, s_sem):
+            self.s, self.base = s_sem, new_recv(H - 1)
+
+        def send(self, i, src, dst):
+            to = nearest[i]
+            r = recv_sem.at[self.base + lax.rem(to - h + H, H) - 1]
+            go(src, dst, (d, t, to), self.s, r)
+
+        def wait(self, name, i, ref):
+            got(name, ref, recv_sem.at[self.base + lax.rem(h - nearest[i] + H, H) - 1])
 
     own_l = local_copy(0, latent, lbuf.at[t, h])
     cb[...] = jnp.zeros(cb.shape, BF16)
     barrier = pltpu.get_barrier_semaphore()
     for kt, kh in peers:
         pl.semaphore_signal(barrier, inc=1, device_id=at(kt, kh), device_id_type=MESH)
-    pl.semaphore_signal(barrier, inc=1, device_id=(pair, t, h), device_id_type=MESH)
-    pl.semaphore_signal(barrier, inc=1, device_id=(across, t, h), device_id_type=MESH)
+    pl.semaphore_signal(barrier, inc=1, device_id=pair_dev, device_id_type=MESH)
+    pl.semaphore_signal(barrier, inc=1, device_id=across_dev, device_id_type=MESH)
+    own_w = local_copy(2, w_b, wb.at[pl.ds(pl.multiple_of((t * H + h) * shard, shard), shard)])
+    own_g = [
+        local_copy(5, gain_in, gall.at[h, pl.ds(0, 1)]),
+        local_copy(6, shift_in, gall.at[h, pl.ds(1, 1)]),
+        local_copy(7, gain_b_in, gain_b), local_copy(8, shift_b_in, shift_b),
+    ]
     own_up = local_copy(1, up_w, upw.at[pl.ds(pl.multiple_of(h * CH, CH), CH)])
-    own_w = local_copy(2, w_b, wb.at[pl.ds(pl.multiple_of((t * H + h) * shard, shard), shard)])
+    own_c = local_copy(4, cot, cb.at[pl.ds(0, F), pl.ds(1, R)])
     own_wl = local_copy(3, w_l, wl)
     abuf[...] = jnp.zeros(abuf.shape, BF16)
     ab[...] = jnp.zeros(ab.shape, BF16)
-    own_c = local_copy(4, cot, cb.at[pl.ds(0, F), pl.ds(1, R)])
-    gall[h] = gain_l[...]
-    sall[h] = shift_l[...]
     own_l.wait()
     with scope("w_barrier"):
         pl.semaphore_wait(barrier, N + 1)
 
-    mine = lbuf.at[t, h]
-    lz = {kh: go(mine, mine, at(0, kh)) for kh in far}
-    gz_in = [go(gain_l, gall.at[h], at(0, kh)) for kh in range(1, H)]
-    gz_in += [go(shift_l, sall.at[h], at(0, kh)) for kh in range(1, H)]
-    ly = [go(mine, mine, at(kt, 0)) for kt in range(1, T)]
-
-    up_rows, up_cols = CH // T, 8 * C2 // 4
-
-    def up_piece(gt, gh, quarter):
+    yes = at(1, 0)
+    w_half = shard // 2
+    half_cols = pl.ds(pl.multiple_of(half * (C2 // 2), C2 // 2), C2 // 2)
+
+    def w_piece(gt, gh, piece_side):
+        start = pl.multiple_of((gt * H + gh) * shard + piece_side * w_half, w_half)
+        return wb.at[pl.ds(start, w_half), half_cols]
+
+    def w_both(gt, gh):
+        return wb.at[pl.ds(pl.multiple_of((gt * H + gh) * shard, shard), shard), half_cols]
+
+    up_rows, up_cols = CH // T, 2 * C2
+
+    def up_piece(gt, gh, n=1):
+        first = 2 * half + (side if n == 1 else 0)
         return upw.at[
             pl.ds(pl.multiple_of(gh * CH + gt * up_rows, up_rows), up_rows),
-            pl.ds(pl.multiple_of(quarter * up_cols, up_cols), up_cols),
+            pl.ds(pl.multiple_of(first * up_cols, up_cols), n * up_cols),
         ]
 
+    mine = lbuf.at[t, h]
+    lz = Along(new_send())
+    ly_s, ly_r = new_send(), new_recv()
+    for i in range(H - 1):
+        lz.send(i, mine, mine)
+    go(mine, mine, yes, ly_s, ly_r)
+    own_w.wait()
+    w_s = new_send()
+    w_mine = w_piece(t, h, side)
+    wy_r = [new_recv() for _ in range(H)]
+    go(w_mine, w_mine, yes, w_s, wy_r[H - 1])
+    for made in own_g:
+        made.wait()
+    gain_s, gain_r = new_send(), new_recv()
+    for kh in range(1, H):
+        go(gall.at[h], gall.at[h], at(0, kh), gain_s, gain_r)
     own_up.wait()
-    uz = {kh: go(up_piece(t, h, q), up_piece(t, h, q), at(0, kh)) for kh in far}
-
-    def back(kh):
-        return lax.rem(h + H - kh, H)
-
-    for kh in range(1, H):
-        recv("w_lz", lz[kh])
-        got = lbuf.at[t, back(kh)]
-        for kt in range(1, T):
-            ly.append(go(got, got, at(kt, 0)))
-
-    ux, upair, uy = [], [], []
-
-    def up_on(gt, gh):
-        piece = up_piece(gt, gh, q)
-        ux.append((gt, gh, go(piece, piece, (across, t, h))))
-        upair.append(go(piece, piece, (pair, t, h)))
-
-    for kh in range(1, H):
-        recv("w_uz", uz[kh])
-        piece = up_piece(t, back(kh), q)
-        for kt in range(1, T):
-            uy.append((kt, kh, go(piece, piece, at(kt, 0))))
-        up_on(t, back(kh))
-
-    recv("w_ly", *ly)
-    recv("w_gain", *gz_in)
+    u_s = new_send()
+    uz = Along(u_s)
+    for i in range(H - 1):
+        uz.send(i, up_piece(t, h), up_piece(t, h))
+
+    for i in range(H - 1):
+        piece = lbuf.at[t, nearest[i]]
+        lz.wait("w_lz", i, piece)
+        go(piece, piece, yes, ly_s, ly_r)
+    left_all(lbuf.at[0, pl.ds(0, H - 1)], lz.s)
+    left_all(lbuf.at[0], ly_s)
+    left_all(gall.at[pl.ds(0, H - 1)], gain_s)
+
+    wx_r, wx_at = [], []
+    wpair_r = new_recv()
+
+    def w_across(gt, gh):
+        wx_r.append(new_recv())
+        wx_at.append((gt, gh))
+        go(w_piece(gt, gh, side), w_piece(gt, gh, side), across_dev, w_s, wx_r[-1])
+
+    def w_pair(k):
+        gt, gh = wx_at[k]
+        got("w_wx", w_piece(gt, gh, 1 - side), wx_r[k])
+        go(w_both(gt, gh), w_both(gt, gh), pair_dev, w_s, wpair_r)
+
+    got("w_wy0", w_piece(1 - t, h, side), wy_r[H - 1])
+    w_across(1 - t, h)
+
+    def halo(buffer, f0, f_two, two_at, step):
+        made = []
+        ok_t_send = (t < T - 1) if step == 1 else (t > 0)
+        ok_t_recv = (t > 0) if step == 1 else (t < T - 1)
+        kt = step % T
+
+        def part_of(fs, n_f, r0, n_r):
+            return buffer.at[pl.ds(fs, n_f), pl.ds(r0, n_r)]
+
+        for kt_, kh_, ok_s, ok_r, src, dst in (
+            (kt, 0, ok_t_send, ok_t_recv, part_of(f_two, 2, 1, R), part_of(two_at, 2, 1, R)),
+            (0, 1, h < H - 1, h > 0, part_of(f0, F, R, 1), part_of(f0, F, 0, 1)),
+            (0, H - 1, h > 0, h < H - 1, part_of(f0, F, 1, 1), part_of(f0, F, R + 1, 1)),
+            (kt, 1, ok_t_send & (h < H - 1), ok_t_recv & (h > 0),
+             part_of(f_two, 2, R, 1), part_of(two_at, 2, 0, 1)),
+            (kt, H - 1, ok_t_send & (h > 0), ok_t_recv & (h < H - 1),
+             part_of(f_two, 2, 1, 1), part_of(two_at, 2, R + 1, 1)),
+        ):
+            c = copy(src, dst, at(kt_, kh_), new_send(), new_recv())
+            pl.when(ok_s)(c.start)
+            made.append((c, ok_s, ok_r))
+        return made
+
+    uy_r = [new_recv() for _ in range(H - 1)]
+    ux_r = [new_recv(), new_recv()]
+    upair_r = new_recv()
+    for i in range(H - 1):
+        piece = up_piece(t, nearest[i])
+        uz.wait("w_uz", i, piece)
+        go(piece, piece, yes, u_s, uy_r[i])
+        go(piece, piece, across_dev, u_s, ux_r[0])
+
+    got("w_ly", lbuf.at[0], ly_r)
+    got("w_gain", gall.at[pl.ds(0, H - 1)], gain_r)
+    wz = Along(w_s)
+    own_c.wait()
+    for i in range(W_EARLY):
+        wz.send(i, w_mine, w_mine)
+    cot_halo = halo(cb, 0, 0, F, -1)
 
     per_l = H * CH // GROUPS
     cells_l = FL * Rl * Cl
@@ -363,7 +458,7 @@
         mean = total[2 * k : 2 * k + 1]
         inv = lax.rsqrt(total[2 * k + 1 : 2 * k + 2] - mean * mean + epsilon)
         x = lbuf[:, k].astype(F32).reshape(cells_l, CH)
-        v = (x - mean) * inv * gall[k] + sall[k]
+        v = (x - mean) * inv * gall[k, 0:1] + gall[k, 1:2]
         lane = k * CH % U
         abuf[k * CH // U, 2 : 2 + FL, 1 : 1 + Rl, :, lane : lane + CH] = (
             (v * jax.nn.sigmoid(v)).astype(BF16).reshape(FL, Rl, Cl, CH)
@@ -401,66 +496,37 @@
         partf[...] = mixed.reshape(FL, Rl, Cl, CH)
         partf[pl.ds(t * Fl, Fl)] += lbuf[t, h].astype(F32)
         part[...] = partf[...].astype(BF16)
-    p_in = []
-    for kt, kh in [(kt, kh) for kh in far + [0] for kt in range(T) if kt or kh]:
+    p_s, p_r = new_send(), new_recv()
+    for kt, kh in peers:
         dev = at(kt, kh)
-        p_in.append(
-            go(part.at[pl.ds(dev[1] * Fl, Fl), pl.ds(dev[2] * band, band)],
-               parts_in.at[kt * H + kh], dev)
-        )
-
-    own_w.wait()
-    own_c.wait()
-    w_half = shard // 2
-
-    def w_piece(gt, gh, piece_side):
-        start = pl.multiple_of((gt * H + gh) * shard + piece_side * w_half, w_half)
-        return wb.at[pl.ds(start, w_half), pl.ds(pl.multiple_of(half * (C2 // 2), C2 // 2), C2 // 2)]
-
-    w_mine = w_piece(t, h, side)
-    wz = {kh: go(w_mine, w_mine, at(0, kh)) for kh in far}
-    wy = [(kt, 0, go(w_mine, w_mine, at(kt, 0))) for kt in range(1, T)]
-    wx, wpair = [], []
-
-    def w_on(gt, gh):
-        piece = w_piece(gt, gh, side)
-        wx.append((gt, gh, go(piece, piece, (across, t, h))))
-        wpair.append(go(piece, piece, (pair, t, h)))
-
-    def halo(buffer, f0, f_two, two_at, step):
-        made = []
-        ok_t_send = (t < T - 1) if step == 1 else (t > 0)
-        ok_t_recv = (t > 0) if step == 1 else (t < T - 1)
-        kt = step % T
-
-        def part_of(fs, n_f, r0, n_r):
-            return buffer.at[pl.ds(fs, n_f), pl.ds(r0, n_r)]
-
-        for kt_, kh_, ok_s, ok_r, src, dst in (
-            (kt, 0, ok_t_send, ok_t_recv, part_of(f_two, 2, 1, R), part_of(two_at, 2, 1, R)),
-            (0, 1, h < H - 1, h > 0, part_of(f0, F, R, 1), part_of(f0, F, 0, 1)),
-            (0, H - 1, h > 0, h < H - 1, part_of(f0, F, 1, 1), part_of(f0, F, R + 1, 1)),
-            (kt, 1, ok_t_send & (h < H - 1), ok_t_recv & (h > 0),
-             part_of(f_two, 2, R, 1), part_of(two_at, 2, 0, 1)),
-            (kt, H - 1, ok_t_send & (h > 0), ok_t_recv & (h < H - 1),
-             part_of(f_two, 2, 1, 1), part_of(two_at, 2, R + 1, 1)),
-        ):
-            c = copy(src, dst, at(kt_, kh_))
-            pl.when(ok_s)(c.start)
-            made.append((c, ok_s, ok_r))
-        return made
-
-    cot_halo = halo(cb, 0, 0, F, -1)
-
-    for kt, kh, made in uy:
-        recv("w_uy", made)
-        up_on(lax.rem(t + T - kt, T), back(kh))
-    for gt, gh, made in ux:
-        recv("w_ux", made)
-        piece = up_piece(gt, gh, lax.rem(q + 2, 4))
-        upair.append(go(piece, piece, (pair, t, h)))
-    recv("w_upair", *upair)
-    recv("w_parts", *p_in)
+        go(part.at[pl.ds(dev[1] * Fl, Fl), pl.ds(dev[2] * band, band)],
+           parts_in.at[kt * H + kh], dev, p_s, p_r)
+    for i in range(W_EARLY, H - 1):
+        wz.send(i, w_mine, w_mine)
+
+    def w_height(i):
+        piece = w_piece(t, nearest[i], side)
+        wz.wait("w_wz", i, piece)
+        go(piece, piece, yes, w_s, wy_r[i])
+        w_across(t, nearest[i])
+
+    for i in range(H - 1):
+        piece = up_piece(1 - t, nearest[i])
+        got("w_uy", piece, uy_r[i])
+        go(piece, piece, across_dev, u_s, ux_r[1])
+    w_height(0)
+    for k in range(2):
+        gt = t if k == 0 else 1 - t
+        got("w_ux", upw.at[pl.ds(0, (H - 1) * up_rows), pl.ds(0, up_cols)], ux_r[k])
+        for i in range(H - 1):
+            piece = up_piece(gt, nearest[i], 2)
+            go(piece, piece, pair_dev, u_s, upair_r)
+    for i in range(1, W_EARLY):
+        w_height(i)
+    got("w_upair", upw.at[pl.ds(0, (H - 1) * CH), pl.ds(0, 4 * C2)], upair_r)
+    got("w_parts", parts_in.at[pl.ds(1, N - 1)], p_r)
+    left_all(parts_in.at[pl.ds(1, N - 1)], p_s)
+    left_all(upw.at[pl.ds(0, (H - 1) * CH)], u_s)
 
     cells_b = Fl * band * Cl
     with scope("c_up"):
@@ -471,7 +537,7 @@
             for kt in range(1, T):
                 value = value + parts_in[kt * H + kh].astype(F32)
             refined = value.reshape(cells_b, CH).astype(BF16)
-            source = back(kh)
+            source = lax.rem(h + H - kh, H)
             expanded = expanded + jnp.dot(
                 refined, upw[pl.ds(pl.multiple_of(source * CH, CH), CH), :],
                 preferred_element_type=F32,
@@ -494,15 +560,14 @@
         up = jnp.concatenate([lace[n] for n in range(C2 // 128)], axis=1)
         stat2[me] = two_rows(jnp.sum(up, 0, keepdims=True), jnp.sum(up * up, 0, keepdims=True))
         ub[2 : 2 + F, 1 : 1 + R] = up.astype(BF16).reshape(F, R, C, C2)
-    s2 = [go(stat2.at[me], stat2.at[me], at(kt, kh)) for kt, kh in peers]
+    s2_s, s2_r = new_send(), new_recv()
+    for kt, kh in peers:
+        go(stat2.at[me], stat2.at[me], at(kt, kh), s2_s, s2_r)
+    left_all(stat2.at[pl.ds(0, N - 1)], s2_s)
     up_halo = halo(ub, 2, F, 0, 1)
 
-    for kh in range(1, H):
-        recv("w_wz", wz[kh])
-        piece = w_piece(t, back(kh), side)
-        for kt in range(1, T):
-            wy.append((kt, kh, go(piece, piece, at(kt, 0))))
-        w_on(t, back(kh))
+    for i in range(W_EARLY, H - 1):
+        w_height(i)
     with scope("w_cothalo"):
         for made, _, ok in cot_halo:
             pl.when(ok)(made.wait_recv)
@@ -511,7 +576,7 @@
     cot3[:, :, :, C2 : 2 * C2] = cb[0:F]
     cot3[:, :, :, 2 * C2 :] = column_shift(wide, C, 1).astype(BF16).reshape(F, R + 2, C, C2)
 
-    recv("w_s2", *s2)
+    got("w_s2", stat2.at[pl.ds(0, N - 1)], s2_r)
     per_b = C2 // GROUPS
     count_b = cells * per_b * N
     total = stat2[0]
@@ -546,15 +611,16 @@
     def ahead(kh):
         return lax.rem(h + kh, H)
 
-    g_y = []
-    for kh in far + [0]:
-        for kt in range(1, T):
-            dev = at(kt, 0)
-            g_y.append((kh, kt, go(g_rows(dev[1], ahead(kh)), gy.at[kt, kh], dev)))
-
-    for kt, kh, made in wy:
-        recv("w_wy", made)
-        w_on(lax.rem(t + T - kt, T), back(kh))
+    order = [*range(H // 2, H), *range(1, H // 2), 0]
+    gy_s, gz_s, gz_r = new_send(), new_send(), new_recv()
+    gy_r = {kh: new_recv() for kh in order}
+    for kh in order:
+        go(g_rows(1 - t, ahead(kh)), gy.at[kh], yes, gy_s, gy_r[kh])
+    left_all(gy, gy_s)
+
+    for i in range(H - 1):
+        got("w_wy", w_piece(1 - t, nearest[i], side), wy_r[i])
+        w_across(1 - t, nearest[i])
     with scope("w_uphalo"):
         for made, _, ok in up_halo:
             pl.when(ok)(made.wait_recv)
@@ -572,45 +638,40 @@
                 v = ub[0:2, rows_at : rows_at + n_rows].astype(F32).reshape(2 * n_rows * C, C2)
                 ab[0:2, rows_at : rows_at + n_rows] = activate(v).reshape(2, n_rows, C, C2)
 
-    for gt, gh, made in wx:
-        recv("w_wx", made)
-        piece = w_piece(gt, gh, 1 - side)
-        wpair.append(go(piece, piece, (pair, t, h)))
-
-    g_z = {}
-
     def g_on(kh):
-        total = None
-        for made_kh, kt, made in g_y:
-            if made_kh == kh:
-                recv("w_gy", made)
-                term = gy[kt, kh].astype(F32)
-                total = term if total is None else total + term
+        got("w_gy", gy.at[kh], gy_r[kh])
         start = pl.multiple_of((t * H + ahead(kh)) * out_rows, out_rows)
-        total = total + gw[pl.ds(start, out_rows), :].astype(F32)
+        total = gy[kh].astype(F32) + gw[pl.ds(start, out_rows), :].astype(F32)
         if kh == 0:
             grad_w[...] = total
         else:
             gs[kh] = total.astype(BF16)
-            g_z[kh] = go(gs.at[kh], gz.at[kh], at(0, kh))
-
-    recv("w_wpair", *wpair)
-
-    acc[...] = jnp.zeros(acc.shape, F32)
-
-    def grad_tap(j, _):
-        lag, dr = j // 3, j % 3
-        win = cb[pl.ds(2 - lag, F), pl.ds(2 - dr, R)].reshape(cells, C2)
-        for dc in range(3):
-            rows = wb[pl.ds(pl.multiple_of((j * 3 + dc) * C2, C2), C2), :]
-            acc[dc] += lax.dot_general(
-                win, rows, (((1,), (1,)), ((), ())), preferred_element_type=F32
+            go(gs.at[kh], gz.at[kh], at(0, kh), gz_s, gz_r)
+
+    for k in range(len(wx_at) - 2):
+        w_pair(k)
+    for k, kh in enumerate(order[:-1]):
+        if k < 2:
+            w_pair(len(wx_at) - 2 + k)
+        g_on(kh)
+    left_all(gs.at[pl.ds(1, H - 1)], gz_s)
+    got("w_wpair", wb.at[pl.ds(0, (N - 1) * shard), pl.ds(0, C2 // 2)], wpair_r)
+    left_all(wb.at[pl.ds(0, (2 * (H - 1) + 1 + 3 * (N - 1)) * w_half // 2)], w_s)
+
+    with scope("c_gradtap"):
+        wide = None
+        for j in range(9):
+            lag, dr = j // 3, j % 3
+            win = cb[2 - lag : 2 - lag + F, 2 - dr : 2 - dr + R].reshape(cells, C2)
+            term = lax.dot_general(
+                win, wb[j * 3 * C2 : (j + 1) * 3 * C2, :], (((1,), (1,)), ((), ())),
+                preferred_element_type=F32,
             )
-        return 0
-
-    with scope("c_gradtap"):
-        lax.fori_loop(0, 9, grad_tap, 0)
-    grad_active = column_shift(acc[0], C, -1) + acc[1] + column_shift(acc[2], C, 1)
+            wide = term if wide is None else wide + term
+        grad_active = (
+            column_shift(wide[:, :C2], C, -1) + wide[:, C2 : 2 * C2]
+            + column_shift(wide[:, 2 * C2 :], C, 1)
+        )
     standard = (ub[2 : 2 + F, 1 : 1 + R].astype(F32).reshape(cells, C2) - mean_b) * inv_b
     std[...] = standard
     normed = standard * gain_b[...] + shift_b[...]
@@ -619,32 +680,31 @@
     stat3[me] = two_rows(
         jnp.sum(grad_normed * standard, 0, keepdims=True), jnp.sum(grad_normed, 0, keepdims=True)
     )
-    s3 = [go(stat3.at[me], stat3.at[me], at(kt, kh)) for kt, kh in peers]
+    s3_s, s3_r = new_send(), new_recv()
+    for kt, kh in peers:
+        go(stat3.at[me], stat3.at[me], at(kt, kh), s3_s, s3_r)
+    left_all(stat3.at[pl.ds(0, N - 1)], s3_s)
     tmp[...] = grad_normed * gain_b[...]
-    for kh in far:
-        g_on(kh)
-
-    acc[0] = jnp.zeros((cells, C2), F32)
-    acc[1] = ub[2 : 2 + F, 1 : 1 + R].astype(F32).reshape(cells, C2)
-    acc[2] = jnp.zeros((cells, C2), F32)
-
-    def tap(j, _):
-        lag, dr = j // 3, j % 3
-        win = ab[pl.ds(lag, F), pl.ds(dr, R)].reshape(cells, C2)
-        for dc in range(3):
-            rows = wb[pl.ds(pl.multiple_of((j * 3 + dc) * C2, C2), C2), :]
-            acc[dc] += jnp.dot(win, rows, preferred_element_type=F32)
-        return 0
 
     with scope("c_tap"):
-        lax.fori_loop(0, 9, tap, 0)
-    decoded[...] = (
-        (column_shift(acc[0], C, 1) + acc[1] + column_shift(acc[2], C, -1))
-        .astype(BF16).reshape(F, R, C, C2)
-    )
+        wide = None
+        for j in range(9):
+            lag, dr = j // 3, j % 3
+            win = ab[lag : lag + F, dr : dr + R].reshape(cells, C2)
+            k3 = jnp.concatenate(
+                [wb[(j * 3 + dc) * C2 : (j * 3 + dc + 1) * C2, :] for dc in range(3)], 1
+            )
+            term = jnp.dot(win, k3, preferred_element_type=F32)
+            wide = term if wide is None else wide + term
+        decoded[...] = (
+            (column_shift(wide[:, :C2], C, 1) + wide[:, C2 : 2 * C2]
+             + column_shift(wide[:, 2 * C2 :], C, -1)
+             + ub[2 : 2 + F, 1 : 1 + R].astype(F32).reshape(cells, C2))
+            .astype(BF16).reshape(F, R, C, C2)
+        )
     g_on(0)
 
-    recv("w_s3", *s3)
+    got("w_s3", stat3.at[pl.ds(0, N - 1)], s3_r)
     total = stat3[0]
     for k in range(1, N):
         total = total + stat3[k]
@@ -655,18 +715,36 @@
         cb[0:F, 1 : 1 + R].astype(F32).reshape(cells, C2) + corrected
     ).astype(BF16).reshape(F, R, C, C2)
 
-    recv("w_gz", *g_z.values())
+    got("w_gz", gz.at[pl.ds(1, H - 1)], gz_r)
     result = grad_w[...]
     for kh in range(1, H):
         result = result + gz[kh].astype(F32)
     grad_w[...] = result
 
     with scope("w_send"):
-        for made in sent:
-            made.wait_send()
+        for ref, s_sem in left:
+            copy(ref, ref, pair_dev, s_sem, recv_sem.at[0]).wait_send()
         for made, ok, _ in cot_halo + up_halo:
             pl.when(ok)(made.wait_send)
-    assert used[0] <= n_send
+    assert counts == [n_send, n_recv], counts
+
+
+def finish_kernel(decoded, grad_up, grad_w, grad_gs, out_d, out_u, out_w, out_g, out_s, sems):
+    moves = [
+        pltpu.make_async_copy(src, dst, sems.at[k])
+        for k, (src, dst) in enumerate((
+            (decoded, out_d), (grad_up, out_u), (grad_w, out_w),
+            (grad_gs.at[pl.ds(0, 1)], out_g), (grad_gs.at[pl.ds(1, 1)], out_s),
+        ))
+    ]
+    for move in moves:
+        move.start()
+    for move in moves:
+        move.wait()
+
+
+def stay(array):
+    return pltpu.with_memory_space_constraint(array, pltpu.HBM)
 
 
 def local_block(shape, *args):
@@ -686,28 +764,30 @@
     if not fits:
         return local(*args)
     sizes = (T, H, Fl, Rl, Cl, CH, C2, F, R, C)
-    n_send = 200
+    n_send = 20
+    n_recv = 20 + 4 * (H - 1) + 2 * H + N - 1
     FL = T * Fl
     band = Rl // H
     cells = F * R * C
     out_rows = 9 * C2 // N
     vmem = pl.BlockSpec(memory_space=pltpu.VMEM)
-    hbm = pl.BlockSpec(memory_space=pl.ANY)
+    hbm = pl.BlockSpec(memory_space=pltpu.HBM)
     flops = 2 * (FL * Rl * Cl * w_l.size + 2 * cells * 27 * C2 * C2 + cells * 9 * C2 * C2)
     outs = pl.pallas_call(
-        functools.partial(block_kernel, sizes, n_send),
+        functools.partial(block_kernel, sizes, n_send, n_recv),
         out_shape=(
             jax.ShapeDtypeStruct(cot.shape, BF16),
             jax.ShapeDtypeStruct(cot.shape, BF16),
             jax.ShapeDtypeStruct((out_rows, C2), F32),
             jax.ShapeDtypeStruct((8, C2), F32),
         ),
-        in_specs=[hbm, vmem, vmem, hbm, hbm, vmem, vmem, hbm, hbm],
+        in_specs=[hbm] * 9,
         out_specs=(vmem,) * 4,
         scratch_shapes=[
             pltpu.VMEM((T, H, Fl, Rl, Cl, CH), BF16),
-            pltpu.VMEM((H, 1, CH), F32),
-            pltpu.VMEM((H, 1, CH), F32),
+            pltpu.VMEM((H, 2, CH), F32),
+            pltpu.VMEM((1, C2), F32),
+            pltpu.VMEM((1, C2), F32),
             pltpu.VMEM(w_l.shape, BF16),
             pltpu.VMEM((T, FL + 2, Rl + 2, Cl, U), BF16),
             pltpu.VMEM((FL, Rl, Cl, CH), BF16),
@@ -723,26 +803,34 @@
             pltpu.VMEM((F + 2, R + 2, C, C2), BF16),
             pltpu.VMEM((F, R + 2, C, 3 * C2), BF16),
             pltpu.VMEM((9 * C2, C2), BF16),
-            pltpu.VMEM((T, H, out_rows, C2), BF16),
             pltpu.VMEM((H, out_rows, C2), BF16),
             pltpu.VMEM((H, out_rows, C2), BF16),
-            pltpu.VMEM((3, cells, C2), F32),
+            pltpu.VMEM((H, out_rows, C2), BF16),
             pltpu.VMEM((cells, C2), F32),
             pltpu.VMEM((C2 // 128, cells, 128), F32),
             pltpu.SemaphoreType.DMA((n_send,)),
-            pltpu.SemaphoreType.DMA((n_send,)),
-            pltpu.SemaphoreType.DMA((5,)),
+            pltpu.SemaphoreType.DMA((n_recv,)),
+            pltpu.SemaphoreType.DMA((9,)),
         ],
         compiler_params=pltpu.CompilerParams(
-            collective_id=0, has_side_effects=True, vmem_limit_bytes=60 * 1024 * 1024
+            collective_id=0, has_side_effects=True, vmem_limit_bytes=VMEM_LIMIT
         ),
         cost_estimate=pl.CostEstimate(flops=flops, bytes_accessed=1 << 23, transcendentals=0),
     )(
-        latent, gain_l.reshape(1, -1), shift_l.reshape(1, -1), w_l, up_w,
-        gain_b.reshape(1, -1), shift_b.reshape(1, -1), w_b, cot,
-    )
-    decoded, grad_up, grad_w, grad_gs = outs
-    return decoded, grad_up, grad_w, grad_gs[0], grad_gs[1]
+        stay(latent), stay(gain_l.reshape(1, -1)), stay(shift_l.reshape(1, -1)), stay(w_l), stay(up_w),
+        stay(gain_b.reshape(1, -1)), stay(shift_b.reshape(1, -1)), stay(w_b), stay(cot),
+    )
+    row = jax.ShapeDtypeStruct((1, C2), F32)
+    done = pl.pallas_call(
+        finish_kernel,
+        out_shape=tuple(jax.ShapeDtypeStruct(a.shape, a.dtype) for a in outs[:3]) + (row, row),
+        in_specs=[vmem] * 4,
+        out_specs=(hbm,) * 5,
+        scratch_shapes=[pltpu.SemaphoreType.DMA((5,))],
+        compiler_params=pltpu.CompilerParams(vmem_limit_bytes=1 << 20),
+        cost_estimate=pl.CostEstimate(flops=0, bytes_accessed=1 << 20, transcendentals=0),
+    )(*outs)
+    return done[0], done[1], done[2], done[3].reshape(C2), done[4].reshape(C2)
 
 
 def solution(mesh):

time: 82.8 us -> 63.4 us (0.77); the launches traced: 81.5 us -> 63.2 us
  Pallas kernels: 74.5 us -> 62.6 us
  local copies, waits for them, and re-layouts: 6.37 us -> 0 us
    pallas_call x1 -> x2, Pallas kernels: 74.5 us -> 62.6 us  [the longest x1 61.6 us: local_block(): pl.pallas_call(functools.partial(block_kernel, sizes, n_send, n_recv), ou...]
    unnamed x3 -> x0, local copies, waits for them, and re-layouts: 5.03 us -> none
    slice x1 -> x0, local copies, waits for them, and re-layouts: 1.34 us -> none  [local_block(): return (decoded, grad_up, grad_w, grad_gs[0], grad_gs[1])]
where the time goes in v2:
time: 63.4 us; the launch traced here: 63.2 us
  Pallas kernels  62.6 us (99%)
  between operations  0.64 us (1%)
    pallas_call x1, Pallas kernels, local_block(): pl.pallas_call(functools.partial(block_kernel, sizes, n_send, n_recv), ou...  61.6 us

profile of v2, /device:TPU:0, one launch (start us, length us, event | category | flops | bytes accessed | tf_op | source)
XLA Modules:
  0.0 63.2 jit_solution(8928466127309125588)
XLA Ops:
  0.6 61.6 %shard_map.128 = (bf16[4,4,32,256]{3,2,1,0:T(8,128)(2,1)S(1)}, bf16[4,4,32,256]{3,2,1,0:T(8,128)(2,1)S(1)}, f32[288,256]{1,0:T(8,128)S(1)}, f32[8,256]{1,0:T(8,128)S(1)}) custom-call(bf16[2,8,16,128]{3,2,1,0:T(8,128)(2,1)} %refs_0_.1, f32[1,128]{1,0:T(1,128)} %bitcast.10, f32[1,128]{1,0:T(1,128)} %bitcast.11, bf16[6912,128]{1,0:T(8,128)(2,1)} %refs_3_.1, ...), custom_call_target="tpu_custom_call" | custom-call | flops 5133828096 | bytes 8388608 | tf_op jit(solution)/shard_map/pallas_call | solution.py:776
  62.3 0.9 %shard_map.129 = (bf16[4,4,32,256]{3,2,1,0:T(8,128)(2,1)}, bf16[4,4,32,256]{3,2,1,0:T(8,128)(2,1)}, f32[288,256]{1,0:T(8,128)}, f32[1,256]{1,0:T(1,128)}, f32[1,256]{1,0:T(1,128)}) custom-call(bf16[4,4,32,256]{3,2,1,0:T(8,128)(2,1)S(1)} %get-tuple-element.14.decoded, bf16[4,4,32,256]{3,2,1,0:T(8,128)(2,1)S(1)} %get-tuple-element.15.grad_up, ...), custom_call_target="tpu_custom_call" | custom-call | bytes 1048576 | tf_op jit(solution)/shard_map/pallas_call | solution.py:824

commit v3 on v2

--- a/solution.py
+++ b/solution.py
@@ -204,7 +204,7 @@
 
 MESH = pl.DeviceIdType.MESH
 VMEM_LIMIT = 32 * 1024 * 1024
-W_EARLY = 2
+CUTS = 2
 F32 = jnp.float32
 BF16 = jnp.bfloat16
 
@@ -297,14 +297,13 @@
         made.start()
         return made
 
-    def near(i):
+    def other(i):
         where = 0
         for hh in range(H):
-            order = sorted((o for o in range(H) if o != hh), key=lambda o: (abs(o - hh), -o))
-            where = where + jnp.where(h == hh, order[i], 0)
+            where = where + jnp.where(h == hh, hh ^ (i + 1), 0)
         return where
 
-    nearest = [near(i) for i in range(H - 1)]
+    nearest = [other(i) for i in range(H - 1)]
 
     class Along:
         def __init__(self, s_sem):
@@ -370,7 +369,7 @@
     w_s = new_send()
     w_mine = w_piece(t, h, side)
     wy_r = [new_recv() for _ in range(H)]
-    go(w_mine, w_mine, yes, w_s, wy_r[H - 1])
+    go(w_both(t, h), w_both(t, h), yes, w_s, wy_r[H - 1])
     for made in own_g:
         made.wait()
     gain_s, gain_r = new_send(), new_recv()
@@ -379,10 +378,17 @@
     own_up.wait()
     u_s = new_send()
     uz = Along(u_s)
+
+    def up_send(core):
+        @pl.when(half == core)
+        def _():
+            for i in range(H - 1):
+                uz.send(i, up_piece(t, h), up_piece(t, h))
+
+    up_send(0)
     for i in range(H - 1):
-        uz.send(i, up_piece(t, h), up_piece(t, h))
-
-    for i in range(H - 1):
+        if i == 2:
+            up_send(1)
         piece = lbuf.at[t, nearest[i]]
         lz.wait("w_lz", i, piece)
         go(piece, piece, yes, ly_s, ly_r)
@@ -403,8 +409,6 @@
         got("w_wx", w_piece(gt, gh, 1 - side), wx_r[k])
         go(w_both(gt, gh), w_both(gt, gh), pair_dev, w_s, wpair_r)
 
-    got("w_wy0", w_piece(1 - t, h, side), wy_r[H - 1])
-    w_across(1 - t, h)
 
     def halo(buffer, f0, f_two, two_at, step):
         made = []
@@ -432,19 +436,21 @@
     uy_r = [new_recv() for _ in range(H - 1)]
     ux_r = [new_recv(), new_recv()]
     upair_r = new_recv()
-    for i in range(H - 1):
+
+    def up_height(i):
         piece = up_piece(t, nearest[i])
         uz.wait("w_uz", i, piece)
         go(piece, piece, yes, u_s, uy_r[i])
         go(piece, piece, across_dev, u_s, ux_r[0])
 
+    up_height(0)
     got("w_ly", lbuf.at[0], ly_r)
     got("w_gain", gall.at[pl.ds(0, H - 1)], gain_r)
+    up_height(1)
     wz = Along(w_s)
     own_c.wait()
-    for i in range(W_EARLY):
-        wz.send(i, w_mine, w_mine)
-    cot_halo = halo(cb, 0, 0, F, -1)
+    wz.send(0, w_mine, w_mine)
+    wz.send(1, w_mine, w_mine)
 
     per_l = H * CH // GROUPS
     cells_l = FL * Rl * Cl
@@ -464,35 +470,44 @@
             (v * jax.nn.sigmoid(v)).astype(BF16).reshape(FL, Rl, Cl, CH)
         )
 
+    up_height(2)
+
     own_wl.wait()
 
-    def window(chunk, tap):
+    parts_of = 2
+    some = FL // parts_of
+
+    def window(m, chunk, tap):
         lag, dr = tap // 9, (tap // 3) % 3
-        return abuf[chunk, pl.ds(lag, FL), pl.ds(dr, Rl)].reshape(cells_l, U)
+        return abuf[chunk, pl.ds(lag + m * some, some), pl.ds(dr, Rl)].reshape(some * Rl * Cl, U)
 
     def w_rows(chunk, tap):
         return wl[pl.ds(pl.multiple_of((tap * T + chunk - 27 * t) * U, U), U), :]
 
     with scope("c_latent"):
-        sums = None
+        sums = [None] * parts_of
         for g in range(4):
             tap = jnp.where(t == 0, 3 * g, 15 + 3 * g)
             for chunk in range(T):
                 k3 = jnp.concatenate([w_rows(chunk, tap + dc) for dc in range(3)], 1)
-                term = jnp.dot(window(chunk, tap), k3, preferred_element_type=F32)
-                sums = term if sums is None else sums + term
+                for m in range(parts_of):
+                    term = jnp.dot(window(m, chunk, tap), k3, preferred_element_type=F32)
+                    sums[m] = term if sums[m] is None else sums[m] + term
         alone = jnp.where(t == 0, 12, 14)
         k2 = jnp.concatenate([w_rows(t, alone), w_rows(t, 13)], 1)
-        both = jnp.dot(window(t, alone), k2, preferred_element_type=F32)
-        lone = both[:, :CH] + jnp.dot(
-            window(1 - t, alone), w_rows(1 - t, alone), preferred_element_type=F32
-        )
-        first = sums[:, :CH] + jnp.where(t == 0, lone, 0.0)
-        last = sums[:, 2 * CH :] + jnp.where(t == 0, 0.0, lone)
-        mixed = (
-            column_shift(first, Cl, 1) + sums[:, CH : 2 * CH] + both[:, CH:]
-            + column_shift(last, Cl, -1)
-        )
+        mixed = []
+        for m in range(parts_of):
+            both = jnp.dot(window(m, t, alone), k2, preferred_element_type=F32)
+            lone = both[:, :CH] + jnp.dot(
+                window(m, 1 - t, alone), w_rows(1 - t, alone), preferred_element_type=F32
+            )
+            first = sums[m][:, :CH] + jnp.where(t == 0, lone, 0.0)
+            last = sums[m][:, 2 * CH :] + jnp.where(t == 0, 0.0, lone)
+            mixed.append(
+                column_shift(first, Cl, 1) + sums[m][:, CH : 2 * CH] + both[:, CH:]
+                + column_shift(last, Cl, -1)
+            )
+        mixed = jnp.concatenate(mixed, 0)
         partf[...] = mixed.reshape(FL, Rl, Cl, CH)
         partf[pl.ds(t * Fl, Fl)] += lbuf[t, h].astype(F32)
         part[...] = partf[...].astype(BF16)
@@ -501,8 +516,8 @@
         dev = at(kt, kh)
         go(part.at[pl.ds(dev[1] * Fl, Fl), pl.ds(dev[2] * band, band)],
            parts_in.at[kt * H + kh], dev, p_s, p_r)
-    for i in range(W_EARLY, H - 1):
-        wz.send(i, w_mine, w_mine)
+    cot_halo = halo(cb, 0, 0, F, -1)
+    wz.send(2, w_mine, w_mine)
 
     def w_height(i):
         piece = w_piece(t, nearest[i], side)
@@ -510,19 +525,27 @@
         go(piece, piece, yes, w_s, wy_r[i])
         w_across(t, nearest[i])
 
+    piece = up_piece(1 - t, nearest[0])
+    got("w_uy", piece, uy_r[0])
+    go(piece, piece, across_dev, u_s, ux_r[1])
+    piece = up_piece(1 - t, nearest[1])
+    got("w_uy", piece, uy_r[1])
+    go(piece, piece, across_dev, u_s, ux_r[1])
+    piece = up_piece(1 - t, nearest[2])
+    got("w_uy", piece, uy_r[2])
+    go(piece, piece, across_dev, u_s, ux_r[1])
+    got("w_wy0", w_both(1 - t, h), wy_r[H - 1])
+    go(w_both(1 - t, h), w_both(1 - t, h), pair_dev, w_s, wpair_r)
+    w_height(0)
+    got("w_ux", upw.at[pl.ds(0, (H - 1) * up_rows), pl.ds(0, up_cols)], ux_r[0])
     for i in range(H - 1):
-        piece = up_piece(1 - t, nearest[i])
-        got("w_uy", piece, uy_r[i])
-        go(piece, piece, across_dev, u_s, ux_r[1])
-    w_height(0)
-    for k in range(2):
-        gt = t if k == 0 else 1 - t
-        got("w_ux", upw.at[pl.ds(0, (H - 1) * up_rows), pl.ds(0, up_cols)], ux_r[k])
-        for i in range(H - 1):
-            piece = up_piece(gt, nearest[i], 2)
-            go(piece, piece, pair_dev, u_s, upair_r)
-    for i in range(1, W_EARLY):
-        w_height(i)
+        piece = up_piece(t, nearest[i], 2)
+        go(piece, piece, pair_dev, u_s, upair_r)
+    got("w_ux", upw.at[pl.ds(0, (H - 1) * up_rows), pl.ds(0, up_cols)], ux_r[1])
+    for i in range(H - 1):
+        piece = up_piece(1 - t, nearest[i], 2)
+        go(piece, piece, pair_dev, u_s, upair_r)
+    w_height(1)
     got("w_upair", upw.at[pl.ds(0, (H - 1) * CH), pl.ds(0, 4 * C2)], upair_r)
     got("w_parts", parts_in.at[pl.ds(1, N - 1)], p_r)
     left_all(parts_in.at[pl.ds(1, N - 1)], p_s)
@@ -566,8 +589,7 @@
     left_all(stat2.at[pl.ds(0, N - 1)], s2_s)
     up_halo = halo(ub, 2, F, 0, 1)
 
-    for i in range(W_EARLY, H - 1):
-        w_height(i)
+    w_height(2)
     with scope("w_cothalo"):
         for made, _, ok in cot_halo:
             pl.when(ok)(made.wait_recv)
@@ -605,22 +627,29 @@
     out_rows = 9 * C2 // N
     y_rows = out_rows * H
 
-    def g_rows(gt, gh):
-        return gw.at[pl.ds(pl.multiple_of((gt * H + gh) * out_rows, out_rows), out_rows)]
+    cut_rows = out_rows // CUTS
+
+    def cut(c):
+        return pl.ds(c * cut_rows, cut_rows)
+
+    def g_at(gt, gh, c):
+        start = (gt * H + gh) * out_rows + c * cut_rows
+        return pl.ds(pl.multiple_of(start, cut_rows), cut_rows)
+
+    def g_rows(gt, gh, c):
+        return gw.at[g_at(gt, gh, c)]
 
     def ahead(kh):
         return lax.rem(h + kh, H)
 
     order = [*range(H // 2, H), *range(1, H // 2), 0]
     gy_s, gz_s, gz_r = new_send(), new_send(), new_recv()
-    gy_r = {kh: new_recv() for kh in order}
+    gy_r = {(kh, c): new_recv() for kh in order for c in range(CUTS)}
     for kh in order:
-        go(g_rows(1 - t, ahead(kh)), gy.at[kh], yes, gy_s, gy_r[kh])
+        for c in range(CUTS):
+            go(g_rows(1 - t, ahead(kh), c), gy.at[kh, cut(c)], yes, gy_s, gy_r[kh, c])
     left_all(gy, gy_s)
 
-    for i in range(H - 1):
-        got("w_wy", w_piece(1 - t, nearest[i], side), wy_r[i])
-        w_across(1 - t, nearest[i])
     with scope("w_uphalo"):
         for made, _, ok in up_halo:
             pl.when(ok)(made.wait_recv)
@@ -638,39 +667,51 @@
                 v = ub[0:2, rows_at : rows_at + n_rows].astype(F32).reshape(2 * n_rows * C, C2)
                 ab[0:2, rows_at : rows_at + n_rows] = activate(v).reshape(2, n_rows, C, C2)
 
-    def g_on(kh):
-        got("w_gy", gy.at[kh], gy_r[kh])
-        start = pl.multiple_of((t * H + ahead(kh)) * out_rows, out_rows)
-        total = gy[kh].astype(F32) + gw[pl.ds(start, out_rows), :].astype(F32)
+    def g_on(kh, c):
+        got("w_gy", gy.at[kh, cut(c)], gy_r[kh, c])
+        total = gy[kh, c * cut_rows : (c + 1) * cut_rows].astype(F32)
+        total = total + gw[g_at(t, ahead(kh), c), :].astype(F32)
         if kh == 0:
-            grad_w[...] = total
+            grad_w[c * cut_rows : (c + 1) * cut_rows] = total
         else:
-            gs[kh] = total.astype(BF16)
-            go(gs.at[kh], gz.at[kh], at(0, kh), gz_s, gz_r)
-
-    for k in range(len(wx_at) - 2):
-        w_pair(k)
-    for k, kh in enumerate(order[:-1]):
-        if k < 2:
-            w_pair(len(wx_at) - 2 + k)
-        g_on(kh)
+            gs[kh, c * cut_rows : (c + 1) * cut_rows] = total.astype(BF16)
+            go(gs.at[kh, cut(c)], gz.at[kh, cut(c)], at(0, kh), gz_s, gz_r)
+
+    steps = [(kh, c) for kh in order for c in range(CUTS)]
+    got("w_wy", w_piece(1 - t, nearest[0], side), wy_r[0])
+    w_across(1 - t, nearest[0])
+    got("w_wy", w_piece(1 - t, nearest[1], side), wy_r[1])
+    w_across(1 - t, nearest[1])
+    got("w_wy", w_piece(1 - t, nearest[2], side), wy_r[2])
+    w_across(1 - t, nearest[2])
+    w_pair(0)
+    w_pair(1)
+    g_on(*steps[0])
+    w_pair(2)
+    g_on(*steps[1])
+    w_pair(3)
+    g_on(*steps[2])
+    w_pair(4)
+    w_pair(5)
     left_all(gs.at[pl.ds(1, H - 1)], gz_s)
     got("w_wpair", wb.at[pl.ds(0, (N - 1) * shard), pl.ds(0, C2 // 2)], wpair_r)
-    left_all(wb.at[pl.ds(0, (2 * (H - 1) + 1 + 3 * (N - 1)) * w_half // 2)], w_s)
+    left_all(wb.at[pl.ds(0, (2 * H + 3 * N - 4) * w_half // 2)], w_s)
 
     with scope("c_gradtap"):
-        wide = None
+        sums = {}
         for j in range(9):
             lag, dr = j // 3, j % 3
             win = cb[2 - lag : 2 - lag + F, 2 - dr : 2 - dr + R].reshape(cells, C2)
-            term = lax.dot_general(
-                win, wb[j * 3 * C2 : (j + 1) * 3 * C2, :], (((1,), (1,)), ((), ())),
-                preferred_element_type=F32,
-            )
-            wide = term if wide is None else wide + term
+            for dc in range(3):
+                term = lax.dot_general(
+                    win, wb[(j * 3 + dc) * C2 : (j * 3 + dc + 1) * C2, :],
+                    (((1,), (1,)), ((), ())), preferred_element_type=F32,
+                )
+                key = (dc, j % 2 if dc == 1 else 0)
+                sums[key] = sums[key] + term if key in sums else term
         grad_active = (
-            column_shift(wide[:, :C2], C, -1) + wide[:, C2 : 2 * C2]
-            + column_shift(wide[:, 2 * C2 :], C, 1)
+            column_shift(sums[0, 0], C, -1) + sums[1, 0] + sums[1, 1]
+            + column_shift(sums[2, 0], C, 1)
         )
     standard = (ub[2 : 2 + F, 1 : 1 + R].astype(F32).reshape(cells, C2) - mean_b) * inv_b
     std[...] = standard
@@ -685,24 +726,30 @@
         go(stat3.at[me], stat3.at[me], at(kt, kh), s3_s, s3_r)
     left_all(stat3.at[pl.ds(0, N - 1)], s3_s)
     tmp[...] = grad_normed * gain_b[...]
-
-    with scope("c_tap"):
-        wide = None
-        for j in range(9):
-            lag, dr = j // 3, j % 3
-            win = ab[lag : lag + F, dr : dr + R].reshape(cells, C2)
-            k3 = jnp.concatenate(
-                [wb[(j * 3 + dc) * C2 : (j * 3 + dc + 1) * C2, :] for dc in range(3)], 1
+    for step in steps[3:4]:
+        g_on(*step)
+
+    some = F // 2
+    n = some * R * C
+    for m in range(2):
+        with scope("c_tap"):
+            wide = None
+            for j in range(9):
+                lag, dr = j // 3, j % 3
+                k3 = jnp.concatenate(
+                    [wb[(j * 3 + dc) * C2 : (j * 3 + dc + 1) * C2, :] for dc in range(3)], 1
+                )
+                win = ab[lag + m * some : lag + (m + 1) * some, dr : dr + R].reshape(n, C2)
+                term = jnp.dot(win, k3, preferred_element_type=F32)
+                wide = term if wide is None else wide + term
+            decoded[m * some : (m + 1) * some] = (
+                (column_shift(wide[:, :C2], C, 1) + wide[:, C2 : 2 * C2]
+                 + column_shift(wide[:, 2 * C2 :], C, -1)
+                 + ub[2 + m * some : 2 + (m + 1) * some, 1 : 1 + R].astype(F32).reshape(n, C2))
+                .astype(BF16).reshape(some, R, C, C2)
             )
-            term = jnp.dot(win, k3, preferred_element_type=F32)
-            wide = term if wide is None else wide + term
-        decoded[...] = (
-            (column_shift(wide[:, :C2], C, 1) + wide[:, C2 : 2 * C2]
-             + column_shift(wide[:, 2 * C2 :], C, -1)
-             + ub[2 : 2 + F, 1 : 1 + R].astype(F32).reshape(cells, C2))
-            .astype(BF16).reshape(F, R, C, C2)
-        )
-    g_on(0)
+        for step in steps[4:6] if m == 0 else steps[6 : -CUTS]:
+            g_on(*step)
 
     got("w_s3", stat3.at[pl.ds(0, N - 1)], s3_r)
     total = stat3[0]
@@ -715,6 +762,8 @@
         cb[0:F, 1 : 1 + R].astype(F32).reshape(cells, C2) + corrected
     ).astype(BF16).reshape(F, R, C, C2)
 
+    for step in steps[-CUTS:]:
+        g_on(*step)
     got("w_gz", gz.at[pl.ds(1, H - 1)], gz_r)
     result = grad_w[...]
     for kh in range(1, H):
@@ -755,17 +804,17 @@
     N = T * H
     U = H * CH // T
     fits = (
-        shape["dp"] % 4 == 0 and T == 2
+        shape["dp"] % 4 == 0 and T == 2 and H & (H - 1) == 0
         and CH % 128 == 0 and U % CH == 0
         and w_b.shape[0] % 32 == 0 and (CH // T) % 16 == 0
-        and (9 * C2) % (16 * N) == 0 and C2 % 256 == 0
+        and (9 * C2) % (16 * CUTS * N) == 0 and C2 % 256 == 0
         and Cl % 16 == 0 and w_l.shape[0] == 27 * U and F >= 2
     )
     if not fits:
         return local(*args)
     sizes = (T, H, Fl, Rl, Cl, CH, C2, F, R, C)
     n_send = 20
-    n_recv = 20 + 4 * (H - 1) + 2 * H + N - 1
+    n_recv = 20 + 4 * (H - 1) + (1 + CUTS) * H + N - 2
     FL = T * Fl
     band = Rl // H
     cells = F * R * C

time: 63.4 us -> 58.8 us (0.927)
  Pallas kernels: 62.6 us -> 57.8 us
    pallas_call x1, Pallas kernels: 61.6 us -> 56.8 us  [local_block(): pl.pallas_call(functools.partial(block_kernel, sizes, n_send, n_recv), ou...]
where the time goes in v3:
time: 58.8 us; the launch traced here: 58.4 us
  Pallas kernels  57.8 us (98%)
  between operations  0.64 us (1%)
    pallas_call x1, Pallas kernels, local_block(): pl.pallas_call(functools.partial(block_kernel, sizes, n_send, n_recv), ou...  56.8 us

profile of v3, /device:TPU:0, one launch (start us, length us, event | category | flops | bytes accessed | tf_op | source)
XLA Modules:
  0.0 58.4 jit_solution(3060883289785677413)
XLA Ops:
  0.6 56.8 %shard_map.128 = (bf16[4,4,32,256]{3,2,1,0:T(8,128)(2,1)S(1)}, bf16[4,4,32,256]{3,2,1,0:T(8,128)(2,1)S(1)}, f32[288,256]{1,0:T(8,128)S(1)}, f32[8,256]{1,0:T(8,128)S(1)}) custom-call(bf16[2,8,16,128]{3,2,1,0:T(8,128)(2,1)} %refs_0_.1, f32[1,128]{1,0:T(1,128)} %bitcast.10, f32[1,128]{1,0:T(1,128)} %bitcast.11, bf16[6912,128]{1,0:T(8,128)(2,1)} %refs_3_.1, ...), custom_call_target="tpu_custom_call" | custom-call | flops 5133828096 | bytes 8388608 | tf_op jit(solution)/shard_map/pallas_call | solution.py:825
  57.5 0.9 %shard_map.129 = (bf16[4,4,32,256]{3,2,1,0:T(8,128)(2,1)}, bf16[4,4,32,256]{3,2,1,0:T(8,128)(2,1)}, f32[288,256]{1,0:T(8,128)}, f32[1,256]{1,0:T(1,128)}, f32[1,256]{1,0:T(1,128)}) custom-call(bf16[4,4,32,256]{3,2,1,0:T(8,128)(2,1)S(1)} %get-tuple-element.14.decoded, bf16[4,4,32,256]{3,2,1,0:T(8,128)(2,1)S(1)} %get-tuple-element.15.grad_up, ...), custom_call_target="tpu_custom_call" | custom-call | bytes 1048576 | tf_op jit(solution)/shard_map/pallas_call | solution.py:873

commit v4 on v3

--- a/solution.py
+++ b/solution.py
@@ -243,7 +243,7 @@
         latent, gain_in, shift_in, w_l, up_w, gain_b_in, shift_b_in, w_b, cot,
         decoded, grad_up, grad_w, grad_gs,
         lbuf, gall, gain_b, shift_b, wl, abuf, part, partf, parts_in, stat2, stat3, upw, wb,
-        ub, std, ab, cb, cot3, gw, gy, gs, gz, tmp, lace, send_sem, recv_sem, local_sem,
+        ub, std, ab, cb, cot3, gw, gy, gf, gs, gz, tmp, lace, send_sem, recv_sem, local_sem,
     ) = refs
     d, t, h = lax.axis_index("dp"), lax.axis_index("tm"), lax.axis_index("height")
     N = T * H
@@ -516,7 +516,6 @@
         dev = at(kt, kh)
         go(part.at[pl.ds(dev[1] * Fl, Fl), pl.ds(dev[2] * band, band)],
            parts_in.at[kt * H + kh], dev, p_s, p_r)
-    cot_halo = halo(cb, 0, 0, F, -1)
     wz.send(2, w_mine, w_mine)
 
     def w_height(i):
@@ -537,6 +536,7 @@
     got("w_wy0", w_both(1 - t, h), wy_r[H - 1])
     go(w_both(1 - t, h), w_both(1 - t, h), pair_dev, w_s, wpair_r)
     w_height(0)
+    cot_halo = halo(cb, 0, 0, F, -1)
     got("w_ux", upw.at[pl.ds(0, (H - 1) * up_rows), pl.ds(0, up_cols)], ux_r[0])
     for i in range(H - 1):
         piece = up_piece(t, nearest[i], 2)
@@ -615,15 +615,19 @@
     with scope("c_gw"):
         own = activate(ub[2 : 2 + F, 1 : 1 + R].astype(F32).reshape(cells, C2))
         ab[2 : 2 + F, 1 : 1 + R] = own.reshape(F, R, C, C2)
-        for dr in range(3):
+        def taps_of(i):
+            dr = jnp.where(t == 0, 2 - i, i)
             term = lax.dot_general(
-                own, cot3[:, 2 - dr : 2 - dr + R].reshape(cells, 3 * C2),
+                own, cot3[:, pl.ds(2 - dr, R)].reshape(cells, 3 * C2),
                 (((0,), (0,)), ((), ())), preferred_element_type=F32,
             )
             for dc in range(3):
-                gw[(dr * 3 + dc) * C2 : (dr * 3 + dc + 1) * C2, :] = (
+                gw[pl.ds(pl.multiple_of((dr * 3 + dc) * C2, C2), C2), :] = (
                     term[:, dc * C2 : (dc + 1) * C2].astype(BF16)
                 )
+
+        taps_of(0)
+        taps_of(1)
     out_rows = 9 * C2 // N
     y_rows = out_rows * H
 
@@ -644,11 +648,25 @@
 
     order = [*range(H // 2, H), *range(1, H // 2), 0]
     gy_s, gz_s, gz_r = new_send(), new_send(), new_recv()
-    gy_r = {(kh, c): new_recv() for kh in order for c in range(CUTS)}
-    for kh in order:
-        for c in range(CUTS):
+    gy_r = {(kh, c): new_recv() for kh in order for c in range(CUTS) if (kh, c) != (1, 0)}
+    first_cut = (1, 0)
+    steps = [(kh, c) for kh in order for c in range(CUTS) if (kh, c) != first_cut]
+    for kh, c in steps:
+        if (kh, c) != (0, 0):
             go(g_rows(1 - t, ahead(kh), c), gy.at[kh, cut(c)], yes, gy_s, gy_r[kh, c])
-    left_all(gy, gy_s)
+    zf_s, zf_r = new_send(), new_recv()
+    go(g_rows(1 - t, ahead(1), 0), gf.at[1], at(0, 1), zf_s, zf_r)
+    with scope("c_gw2"):
+        taps_of(2)
+    go(g_rows(t, ahead(1), 0), gf.at[0], at(0, 1), zf_s, zf_r)
+    left_all(gw.at[pl.ds(0, len(steps) * cut_rows)], gy_s)
+    left_all(gf, zf_s)
+
+    def g_join():
+        got("w_gf", gf, zf_r)
+        total = gw[g_at(1 - t, h, 0), :].astype(F32) + gf[1].astype(F32)
+        gs[0, :cut_rows] = total.astype(BF16)
+        go(gs.at[0, cut(0)], gy.at[0, cut(0)], yes, gy_s, gy_r[0, 0])
 
     with scope("w_uphalo"):
         for made, _, ok in up_halo:
@@ -671,13 +689,14 @@
         got("w_gy", gy.at[kh, cut(c)], gy_r[kh, c])
         total = gy[kh, c * cut_rows : (c + 1) * cut_rows].astype(F32)
         total = total + gw[g_at(t, ahead(kh), c), :].astype(F32)
+        if (kh, c) == (0, 0):
+            total = total + gf[0].astype(F32)
         if kh == 0:
             grad_w[c * cut_rows : (c + 1) * cut_rows] = total
         else:
             gs[kh, c * cut_rows : (c + 1) * cut_rows] = total.astype(BF16)
             go(gs.at[kh, cut(c)], gz.at[kh, cut(c)], at(0, kh), gz_s, gz_r)
 
-    steps = [(kh, c) for kh in order for c in range(CUTS)]
     got("w_wy", w_piece(1 - t, nearest[0], side), wy_r[0])
     w_across(1 - t, nearest[0])
     got("w_wy", w_piece(1 - t, nearest[1], side), wy_r[1])
@@ -691,9 +710,11 @@
     g_on(*steps[1])
     w_pair(3)
     g_on(*steps[2])
+    g_join()
     w_pair(4)
     w_pair(5)
-    left_all(gs.at[pl.ds(1, H - 1)], gz_s)
+    g_on(*steps[3])
+    left_all(gw.at[pl.ds(0, (len(steps) - CUTS) * cut_rows)], gz_s)
     got("w_wpair", wb.at[pl.ds(0, (N - 1) * shard), pl.ds(0, C2 // 2)], wpair_r)
     left_all(wb.at[pl.ds(0, (2 * H + 3 * N - 4) * w_half // 2)], w_s)
 
@@ -726,7 +747,7 @@
         go(stat3.at[me], stat3.at[me], at(kt, kh), s3_s, s3_r)
     left_all(stat3.at[pl.ds(0, N - 1)], s3_s)
     tmp[...] = grad_normed * gain_b[...]
-    for step in steps[3:4]:
+    for step in steps[4:5]:
         g_on(*step)
 
     some = F // 2
@@ -748,7 +769,7 @@
                  + ub[2 + m * some : 2 + (m + 1) * some, 1 : 1 + R].astype(F32).reshape(n, C2))
                 .astype(BF16).reshape(some, R, C, C2)
             )
-        for step in steps[4:6] if m == 0 else steps[6 : -CUTS]:
+        for step in steps[5:5] if m == 0 else steps[5 : -CUTS]:
             g_on(*step)
 
     got("w_s3", stat3.at[pl.ds(0, N - 1)], s3_r)
@@ -764,11 +785,14 @@
 
     for step in steps[-CUTS:]:
         g_on(*step)
-    got("w_gz", gz.at[pl.ds(1, H - 1)], gz_r)
-    result = grad_w[...]
-    for kh in range(1, H):
-        result = result + gz[kh].astype(F32)
-    grad_w[...] = result
+    got("w_gz", gw.at[pl.ds(0, (len(steps) - CUTS) * cut_rows)], gz_r)
+    for c in range(CUTS):
+        rows = slice(c * cut_rows, (c + 1) * cut_rows)
+        result = grad_w[rows]
+        for kh in range(1, H):
+            if (kh, c) != first_cut:
+                result = result + gz[kh, rows].astype(F32)
+        grad_w[rows] = result
 
     with scope("w_send"):
         for ref, s_sem in left:
@@ -804,7 +828,7 @@
     N = T * H
     U = H * CH // T
     fits = (
-        shape["dp"] % 4 == 0 and T == 2 and H & (H - 1) == 0
+        shape["dp"] % 4 == 0 and T == 2 and H == 4
         and CH % 128 == 0 and U % CH == 0
         and w_b.shape[0] % 32 == 0 and (CH // T) % 16 == 0
         and (9 * C2) % (16 * CUTS * N) == 0 and C2 % 256 == 0
@@ -813,7 +837,7 @@
     if not fits:
         return local(*args)
     sizes = (T, H, Fl, Rl, Cl, CH, C2, F, R, C)
-    n_send = 20
+    n_send = 21
     n_recv = 20 + 4 * (H - 1) + (1 + CUTS) * H + N - 2
     FL = T * Fl
     band = Rl // H
@@ -853,6 +877,7 @@
             pltpu.VMEM((F, R + 2, C, 3 * C2), BF16),
             pltpu.VMEM((9 * C2, C2), BF16),
             pltpu.VMEM((H, out_rows, C2), BF16),
+            pltpu.VMEM((2, out_rows // CUTS, C2), BF16),
             pltpu.VMEM((H, out_rows, C2), BF16),
             pltpu.VMEM((H, out_rows, C2), BF16),
             pltpu.VMEM((cells, C2), F32),

time: 58.8 us -> 57.9 us (0.985)
  Pallas kernels: 57.8 us -> 57.1 us
    pallas_call x1, Pallas kernels: 56.8 us -> 56.2 us  [local_block(): pl.pallas_call(functools.partial(block_kernel, sizes, n_send, n_recv), ou...]
where the time goes in v4:
time: 57.9 us; the launch traced here: 57.8 us
  Pallas kernels  57.1 us (99%)
  between operations  0.64 us (1%)
    pallas_call x1, Pallas kernels, local_block(): pl.pallas_call(functools.partial(block_kernel, sizes, n_send, n_recv), ou...  56.2 us

profile of v4, /device:TPU:0, one launch (start us, length us, event | category | flops | bytes accessed | tf_op | source)
XLA Modules:
  0.0 57.8 jit_solution(1037655343929101999)
XLA Ops:
  0.6 56.2 %shard_map.128 = (bf16[4,4,32,256]{3,2,1,0:T(8,128)(2,1)S(1)}, bf16[4,4,32,256]{3,2,1,0:T(8,128)(2,1)S(1)}, f32[288,256]{1,0:T(8,128)S(1)}, f32[8,256]{1,0:T(8,128)S(1)}) custom-call(bf16[2,8,16,128]{3,2,1,0:T(8,128)(2,1)} %refs_0_.1, f32[1,128]{1,0:T(1,128)} %bitcast.10, f32[1,128]{1,0:T(1,128)} %bitcast.11, bf16[6912,128]{1,0:T(8,128)(2,1)} %refs_3_.1, ...), custom_call_target="tpu_custom_call" | custom-call | flops 5133828096 | bytes 8388608 | tf_op jit(solution)/shard_map/pallas_call | solution.py:849
  56.8 0.9 %shard_map.129 = (bf16[4,4,32,256]{3,2,1,0:T(8,128)(2,1)}, bf16[4,4,32,256]{3,2,1,0:T(8,128)(2,1)}, f32[288,256]{1,0:T(8,128)}, f32[1,256]{1,0:T(1,128)}, f32[1,256]{1,0:T(1,128)}) custom-call(bf16[4,4,32,256]{3,2,1,0:T(8,128)(2,1)S(1)} %get-tuple-element.14.decoded, bf16[4,4,32,256]{3,2,1,0:T(8,128)(2,1)S(1)} %get-tuple-element.15.grad_up, ...), custom_call_target="tpu_custom_call" | custom-call | bytes 1048576 | tf_op jit(solution)/shard_map/pallas_call | solution.py:898

commit v5 on v4

--- a/solution.py
+++ b/solution.py
@@ -237,6 +237,10 @@
     return jnp.where(row == 0, first, jnp.where(row == 1, second, 0.0))
 
 
+def side_by_side(first, second):
+    return jnp.concatenate([first, second], 1)
+
+
 def block_kernel(sizes, n_send, n_recv, *refs):
     (T, H, Fl, Rl, Cl, CH, C2, F, R, C) = sizes
     (
@@ -533,14 +537,14 @@
     piece = up_piece(1 - t, nearest[2])
     got("w_uy", piece, uy_r[2])
     go(piece, piece, across_dev, u_s, ux_r[1])
-    got("w_wy0", w_both(1 - t, h), wy_r[H - 1])
-    go(w_both(1 - t, h), w_both(1 - t, h), pair_dev, w_s, wpair_r)
     w_height(0)
     cot_halo = halo(cb, 0, 0, F, -1)
     got("w_ux", upw.at[pl.ds(0, (H - 1) * up_rows), pl.ds(0, up_cols)], ux_r[0])
     for i in range(H - 1):
         piece = up_piece(t, nearest[i], 2)
         go(piece, piece, pair_dev, u_s, upair_r)
+    got("w_wy0", w_both(1 - t, h), wy_r[H - 1])
+    go(w_both(1 - t, h), w_both(1 - t, h), pair_dev, w_s, wpair_r)
     got("w_ux", upw.at[pl.ds(0, (H - 1) * up_rows), pl.ds(0, up_cols)], ux_r[1])
     for i in range(H - 1):
         piece = up_piece(1 - t, nearest[i], 2)
@@ -581,7 +585,7 @@
         cells = F * R * C
         me = t * H + h
         up = jnp.concatenate([lace[n] for n in range(C2 // 128)], axis=1)
-        stat2[me] = two_rows(jnp.sum(up, 0, keepdims=True), jnp.sum(up * up, 0, keepdims=True))
+        stat2[me] = side_by_side(jnp.sum(up, 0, keepdims=True), jnp.sum(up * up, 0, keepdims=True))
         ub[2 : 2 + F, 1 : 1 + R] = up.astype(BF16).reshape(F, R, C, C2)
     s2_s, s2_r = new_send(), new_recv()
     for kt, kh in peers:
@@ -590,6 +594,8 @@
     up_halo = halo(ub, 2, F, 0, 1)
 
     w_height(2)
+    got("w_wy", w_piece(1 - t, nearest[0], side), wy_r[0])
+    w_across(1 - t, nearest[0])
     with scope("w_cothalo"):
         for made, _, ok in cot_halo:
             pl.when(ok)(made.wait_recv)
@@ -598,13 +604,15 @@
     cot3[:, :, :, C2 : 2 * C2] = cb[0:F]
     cot3[:, :, :, 2 * C2 :] = column_shift(wide, C, 1).astype(BF16).reshape(F, R + 2, C, C2)
 
+    got("w_wy", w_piece(1 - t, nearest[1], side), wy_r[1])
+    w_across(1 - t, nearest[1])
     got("w_s2", stat2.at[pl.ds(0, N - 1)], s2_r)
     per_b = C2 // GROUPS
     count_b = cells * per_b * N
     total = stat2[0]
     for k in range(1, N):
         total = total + stat2[k]
-    total = over_groups(total, per_b) / count_b
+    total = over_groups(jnp.concatenate([total[:, :C2], total[:, C2:]], 0), per_b) / count_b
     mean_b = total[0:1]
     inv_b = lax.rsqrt(total[1:2] - mean_b * mean_b + epsilon)
 
@@ -697,10 +705,6 @@
             gs[kh, c * cut_rows : (c + 1) * cut_rows] = total.astype(BF16)
             go(gs.at[kh, cut(c)], gz.at[kh, cut(c)], at(0, kh), gz_s, gz_r)
 
-    got("w_wy", w_piece(1 - t, nearest[0], side), wy_r[0])
-    w_across(1 - t, nearest[0])
-    got("w_wy", w_piece(1 - t, nearest[1], side), wy_r[1])
-    w_across(1 - t, nearest[1])
     got("w_wy", w_piece(1 - t, nearest[2], side), wy_r[2])
     w_across(1 - t, nearest[2])
     w_pair(0)
@@ -708,12 +712,10 @@
     g_on(*steps[0])
     w_pair(2)
     g_on(*steps[1])
+    g_join()
     w_pair(3)
-    g_on(*steps[2])
-    g_join()
     w_pair(4)
     w_pair(5)
-    g_on(*steps[3])
     left_all(gw.at[pl.ds(0, (len(steps) - CUTS) * cut_rows)], gz_s)
     got("w_wpair", wb.at[pl.ds(0, (N - 1) * shard), pl.ds(0, C2 // 2)], wpair_r)
     left_all(wb.at[pl.ds(0, (2 * H + 3 * N - 4) * w_half // 2)], w_s)
@@ -739,7 +741,7 @@
     normed = standard * gain_b[...] + shift_b[...]
     sigmoid = jax.nn.sigmoid(normed)
     grad_normed = grad_active * sigmoid * (1.0 + normed * (1.0 - sigmoid))
-    stat3[me] = two_rows(
+    stat3[me] = side_by_side(
         jnp.sum(grad_normed * standard, 0, keepdims=True), jnp.sum(grad_normed, 0, keepdims=True)
     )
     s3_s, s3_r = new_send(), new_recv()
@@ -747,7 +749,7 @@
         go(stat3.at[me], stat3.at[me], at(kt, kh), s3_s, s3_r)
     left_all(stat3.at[pl.ds(0, N - 1)], s3_s)
     tmp[...] = grad_normed * gain_b[...]
-    for step in steps[4:5]:
+    for step in steps[2:5]:
         g_on(*step)
 
     some = F // 2
@@ -776,6 +778,7 @@
     total = stat3[0]
     for k in range(1, N):
         total = total + stat3[k]
+    total = two_rows(total[:, :C2], total[:, C2:])
     grad_gs[...] = total
     means = over_groups(total * gain_b[...], per_b) / count_b
     corrected = (tmp[...] - means[1:2] - std[...] * means[0:1]) * inv_b
@@ -866,8 +869,8 @@
             pltpu.VMEM((FL, Rl, Cl, CH), BF16),
             pltpu.VMEM((FL, Rl, Cl, CH), F32),
             pltpu.VMEM((N, Fl, band, Cl, CH), BF16),
-            pltpu.VMEM((N, 8, C2), F32),
-            pltpu.VMEM((N, 8, C2), F32),
+            pltpu.VMEM((N, 1, 2 * C2), F32),
+            pltpu.VMEM((N, 1, 2 * C2), F32),
             pltpu.VMEM((H * CH, 8 * C2), BF16),
             pltpu.VMEM((27 * C2, C2), BF16),
             pltpu.VMEM((F + 2, R + 2, C, C2), BF16),

time: 57.9 us -> 55.3 us (0.955)
  Pallas kernels: 57.1 us -> 54.5 us
    pallas_call x1, Pallas kernels: 56.2 us -> 53.5 us  [local_block(): pl.pallas_call(functools.partial(block_kernel, sizes, n_send, n_recv), ou...]
where the time goes in v5:
time: 55.3 us; the launch traced here: 55.1 us
  Pallas kernels  54.5 us (99%)
  between operations  0.64 us (1%)
    pallas_call x1, Pallas kernels, local_block(): pl.pallas_call(functools.partial(block_kernel, sizes, n_send, n_recv), ou...  53.5 us

profile of v5, /device:TPU:0, one launch (start us, length us, event | category | flops | bytes accessed | tf_op | source)
XLA Modules:
  0.0 55.1 jit_solution(17553985894573132589)
XLA Ops:
  0.6 53.5 %shard_map.128 = (bf16[4,4,32,256]{3,2,1,0:T(8,128)(2,1)S(1)}, bf16[4,4,32,256]{3,2,1,0:T(8,128)(2,1)S(1)}, f32[288,256]{1,0:T(8,128)S(1)}, f32[8,256]{1,0:T(8,128)S(1)}) custom-call(bf16[2,8,16,128]{3,2,1,0:T(8,128)(2,1)} %refs_0_.1, f32[1,128]{1,0:T(1,128)} %bitcast.10, f32[1,128]{1,0:T(1,128)} %bitcast.11, bf16[6912,128]{1,0:T(8,128)(2,1)} %refs_3_.1, ...), custom_call_target="tpu_custom_call" | custom-call | flops 5133828096 | bytes 8388608 | tf_op jit(solution)/shard_map/pallas_call | solution.py:852
  54.2 0.9 %shard_map.129 = (bf16[4,4,32,256]{3,2,1,0:T(8,128)(2,1)}, bf16[4,4,32,256]{3,2,1,0:T(8,128)(2,1)}, f32[288,256]{1,0:T(8,128)}, f32[1,256]{1,0:T(1,128)}, f32[1,256]{1,0:T(1,128)}) custom-call(bf16[4,4,32,256]{3,2,1,0:T(8,128)(2,1)S(1)} %get-tuple-element.14.decoded, bf16[4,4,32,256]{3,2,1,0:T(8,128)(2,1)S(1)} %get-tuple-element.15.grad_up, ...), custom_call_target="tpu_custom_call" | custom-call | bytes 1048576 | tf_op jit(solution)/shard_map/pallas_call | solution.py:901

commit v6 on v5

--- a/solution.py
+++ b/solution.py
@@ -337,8 +337,6 @@
     own_up = local_copy(1, up_w, upw.at[pl.ds(pl.multiple_of(h * CH, CH), CH)])
     own_c = local_copy(4, cot, cb.at[pl.ds(0, F), pl.ds(1, R)])
     own_wl = local_copy(3, w_l, wl)
-    abuf[...] = jnp.zeros(abuf.shape, BF16)
-    ab[...] = jnp.zeros(ab.shape, BF16)
     own_l.wait()
     with scope("w_barrier"):
         pl.semaphore_wait(barrier, N + 1)
@@ -390,6 +388,8 @@
                 uz.send(i, up_piece(t, h), up_piece(t, h))
 
     up_send(0)
+    abuf[...] = jnp.zeros(abuf.shape, BF16)
+    ab[...] = jnp.zeros(ab.shape, BF16)
     for i in range(H - 1):
         if i == 2:
             up_send(1)
@@ -438,7 +438,8 @@
         return made
 
     uy_r = [new_recv() for _ in range(H - 1)]
-    ux_r = [new_recv(), new_recv()]
+    ux_r = [new_recv()]
+    ux_last_r = [new_recv() for _ in range(H - 1)]
     upair_r = new_recv()
 
     def up_height(i):
@@ -530,13 +531,13 @@
 
     piece = up_piece(1 - t, nearest[0])
     got("w_uy", piece, uy_r[0])
-    go(piece, piece, across_dev, u_s, ux_r[1])
+    go(piece, piece, across_dev, u_s, ux_last_r[0])
     piece = up_piece(1 - t, nearest[1])
     got("w_uy", piece, uy_r[1])
-    go(piece, piece, across_dev, u_s, ux_r[1])
+    go(piece, piece, across_dev, u_s, ux_last_r[1])
     piece = up_piece(1 - t, nearest[2])
     got("w_uy", piece, uy_r[2])
-    go(piece, piece, across_dev, u_s, ux_r[1])
+    go(piece, piece, across_dev, u_s, ux_last_r[2])
     w_height(0)
     cot_halo = halo(cb, 0, 0, F, -1)
     got("w_ux", upw.at[pl.ds(0, (H - 1) * up_rows), pl.ds(0, up_cols)], ux_r[0])
@@ -545,8 +546,8 @@
         go(piece, piece, pair_dev, u_s, upair_r)
     got("w_wy0", w_both(1 - t, h), wy_r[H - 1])
     go(w_both(1 - t, h), w_both(1 - t, h), pair_dev, w_s, wpair_r)
-    got("w_ux", upw.at[pl.ds(0, (H - 1) * up_rows), pl.ds(0, up_cols)], ux_r[1])
     for i in range(H - 1):
+        got("w_ux", up_piece(1 - t, nearest[i]), ux_last_r[i])
         piece = up_piece(1 - t, nearest[i], 2)
         go(piece, piece, pair_dev, u_s, upair_r)
     w_height(1)
@@ -841,7 +842,7 @@
         return local(*args)
     sizes = (T, H, Fl, Rl, Cl, CH, C2, F, R, C)
     n_send = 21
-    n_recv = 20 + 4 * (H - 1) + (1 + CUTS) * H + N - 2
+    n_recv = 19 + 5 * (H - 1) + (1 + CUTS) * H + N - 2
     FL = T * Fl
     band = Rl // H
     cells = F * R * C

time: 55.3 us -> 54.5 us (0.986)
  Pallas kernels: 54.5 us -> 53.3 us
    pallas_call x1, Pallas kernels: 53.5 us -> 52.3 us  [local_block(): pl.pallas_call(functools.partial(block_kernel, sizes, n_send, n_recv), ou...]
where the time goes in v6:
time: 54.5 us; the launch traced here: 53.9 us
  Pallas kernels  53.3 us (98%)
  between operations  0.64 us (1%)
    pallas_call x1, Pallas kernels, local_block(): pl.pallas_call(functools.partial(block_kernel, sizes, n_send, n_recv), ou...  52.3 us

profile of v6, /device:TPU:0, one launch (start us, length us, event | category | flops | bytes accessed | tf_op | source)
XLA Modules:
  0.0 53.9 jit_solution(17737323088462971753)
XLA Ops:
  0.6 52.3 %shard_map.128 = (bf16[4,4,32,256]{3,2,1,0:T(8,128)(2,1)S(1)}, bf16[4,4,32,256]{3,2,1,0:T(8,128)(2,1)S(1)}, f32[288,256]{1,0:T(8,128)S(1)}, f32[8,256]{1,0:T(8,128)S(1)}) custom-call(bf16[2,8,16,128]{3,2,1,0:T(8,128)(2,1)} %refs_0_.1, f32[1,128]{1,0:T(1,128)} %bitcast.10, f32[1,128]{1,0:T(1,128)} %bitcast.11, bf16[6912,128]{1,0:T(8,128)(2,1)} %refs_3_.1, ...), custom_call_target="tpu_custom_call" | custom-call | flops 5133828096 | bytes 8388608 | tf_op jit(solution)/shard_map/pallas_call | solution.py:853
  53.0 0.9 %shard_map.129 = (bf16[4,4,32,256]{3,2,1,0:T(8,128)(2,1)}, bf16[4,4,32,256]{3,2,1,0:T(8,128)(2,1)}, f32[288,256]{1,0:T(8,128)}, f32[1,256]{1,0:T(1,128)}, f32[1,256]{1,0:T(1,128)}) custom-call(bf16[4,4,32,256]{3,2,1,0:T(8,128)(2,1)S(1)} %get-tuple-element.14.decoded, bf16[4,4,32,256]{3,2,1,0:T(8,128)(2,1)S(1)} %get-tuple-element.15.grad_up, ...), custom_call_target="tpu_custom_call" | custom-call | bytes 1048576 | tf_op jit(solution)/shard_map/pallas_call | solution.py:902
